TPU v7x, 32 devices: a whole 2x2x4 slice. The times are simulated.
32 devices in a mesh: pi: 4 (over y, x), pj: 8 (over z, core).
Axes of the slice: x: 2, y: 2, z: 4, core: 2. Of those that a mesh axis runs over, the one named last changes fastest.
Arguments:
- duo_embedding: bfloat16 [1024, 1024, 128], P('pi', 'pj'), may hold values from -12 to 12
- duo_attention_weights: float32 [128, 8], replicated, may hold values from -16 to 16
- aligned_embedding: bfloat16 [256, 64, 1024], P('pj', None, 'pi'), may hold values from -6 to 6
- aligned_scaling_weights: float32 [64], replicated, may hold values from 0.5 to 1.5
- aligned_shift_vector: float32 [64], replicated, may hold values from -3 to 3
- payload_weights: bfloat16 [64, 256], replicated, may hold values from -0.75 to 0.75
- switch_weights: bfloat16 [64, 256], replicated, may hold values from -0.75 to 0.75
- closing_weights: bfloat16 [256, 64], replicated, may hold values from -1.5 to 1.5
Outputs:
- update: bfloat16 [256, 64, 1024], P('pj', None, 'pi')
All inputs are finite; a program needn't handle non-finite values.
Results may differ from a plain program's by a relative error of at most 0.009.
Values may be sent and summed in bfloat16 or wider, within the bound.
A program may use at most 192 MiB of HBM per device.

v0:
```python
import functools

import jax
import jax.numpy as jnp
from jax import lax
from jax.experimental import pallas as pl
from jax.experimental.pallas import tpu as pltpu
from jax.sharding import PartitionSpec as P

EPS = 1e-05
MESH = pl.DeviceIdType.MESH
NT = (((1,), (1,)), ((), ()))
CORES = 2
TILE = 16
CHUNK = 32
LAG = 3
GROUP = 8


def dot(a, b, dims=(((1,), (0,)), ((), ()))):
    return lax.dot_general(a, b, dims, preferred_element_type=jnp.float32)


def split_weights(w):
    w = w - jnp.mean(w, axis=1, keepdims=True)
    hi = w.astype(jnp.bfloat16).astype(jnp.float32)
    mid = (w - hi).astype(jnp.bfloat16).astype(jnp.float32)
    w3 = jnp.concatenate([hi, mid, w - hi - mid, jnp.zeros_like(w)], axis=0)
    return w3.astype(jnp.bfloat16)


def tile_scores(x, w3):
    rows, cols, chans = x.shape
    heads = w3.shape[0] // 4
    x = x.reshape(rows * cols, chans)
    mean = dot(x, jnp.ones((chans, chans), jnp.bfloat16)) * (1.0 / chans)
    centred = x.astype(jnp.float32) - mean
    square = centred * centred
    top = square.astype(jnp.bfloat16)
    rest = (square - top.astype(jnp.float32)).astype(jnp.bfloat16)
    ones = jnp.ones((2 * heads, 2 * chans), jnp.bfloat16)
    variance = dot(ones, jnp.concatenate([top, rest], axis=1), NT)[:heads] * (1.0 / chans)
    parts = dot(w3, x, NT)
    scores = parts[:heads] + (parts[heads : 2 * heads] + parts[2 * heads : 3 * heads])
    return scores * lax.rsqrt(variance + EPS)


def kernel(
    pi_count,
    pj_count,
    pair_hbm,
    w_ref,
    msa_hbm,
    gain_ref,
    shift_ref,
    wv_ref,
    ws_ref,
    wc_ref,
    out_ref,
    pair,
    msa,
    ex,
    hold,
    peaks,
    scale,
    vals,
    weights,
    acc,
    gate,
    pair_sem,
    msa_sem,
    ex_rs,
    ex_fw,
    ex_dn,
    ex_pt,
    pk_rs,
    pk_ss,
    ms_rs,
    ms_sx,
    ms_up,
    ms_dn,
):
    me_i, me_j = lax.axis_index("pi"), lax.axis_index("pj")
    line, yline = pj_count // CORES, pi_count // 2
    z, core = me_j // CORES, me_j % CORES
    y, x = me_i // 2, me_i % 2
    chunks = ex.shape[1]
    heads, cols = ex.shape[2], ex.shape[4]
    rows = chunks * CHUNK
    seqs, chans = msa.shape[1], msa.shape[2]
    half = seqs // 2
    span = vals.shape[1] - 16
    width = span // seqs
    mate = me_j - core + (1 - core)
    x_near = me_i - x + (1 - x)

    pair_in = lambda q: pltpu.make_async_copy(
        pair_hbm.at[pl.ds(q * CHUNK, CHUNK)], pair.at[q], pair_sem.at[q]
    )
    own_in = pltpu.make_async_copy(msa_hbm, msa.at[me_i], msa_sem)
    own_in.start()
    lax.fori_loop(0, chunks, lambda q, c: (pair_in(q).start(), c)[1], 0)

    barrier = pltpu.get_barrier_semaphore()

    def greet(i, j):
        pl.semaphore_signal(barrier, inc=1, device_id=(i, j), device_id_type=MESH)

    lax.fori_loop(1, pj_count, lambda r, c: (greet(me_i, (me_j + r) % pj_count), c)[1], 0)
    greet(x_near, me_j)
    up_y, down_y = y < yline - 1, y > 0
    pl.when(up_y)(lambda: greet(me_i + 2, me_j))
    pl.when(down_y)(lambda: greet(me_i - 2, me_j))
    pl.semaphore_wait(barrier, pj_count + jnp.where(up_y, 1, 0) + jnp.where(down_y, 1, 0))

    def part(p, h):
        return msa.at[p, pl.ds(h * half, half)]

    def msa_copy(p, h, send, i):
        return pltpu.make_async_remote_copy(
            part(p, h), part(p, h), send.at[p, h], ms_rs.at[p, h],
            device_id=(i, me_j), device_id_type=MESH,
        )

    def to_x(p, h):
        return msa_copy(p, h, ms_sx, x_near)

    def to_up(p, h):
        return msa_copy(p, h, ms_up, me_i + 2)

    def to_down(p, h):
        return msa_copy(p, h, ms_dn, me_i - 2)

    def along_y(p, h):
        pl.when(up_y)(lambda: to_up(p, h).start())
        pl.when(down_y)(lambda: to_down(p, h).start())

    def take(p, h):
        to_x(p, h).wait_recv()

    own_in.wait()
    to_x(me_i, 0).start()
    along_y(me_i, 1)
    to_x(me_i, 1).start()
    along_y(me_i, 0)

    def pass_y(e, column, h, cross):
        below, above = me_i - x + column - 2 * e, me_i - x + column + 2 * e

        @pl.when(y - e >= 0)
        def _():
            take(below, h)
            pl.when(up_y)(lambda: to_up(below, h).start())
            if cross:
                to_x(below, h).start()

        @pl.when(y + e < yline)
        def _():
            take(above, h)
            pl.when(down_y)(lambda: to_down(above, h).start())
            if cross:
                to_x(above, h).start()

    def first_relays():
        take(x_near, 0)
        along_y(x_near, 0)
        for e in range(1, yline):
            pass_y(e, x, 1, True)

    def ex_copy(o, q, send, j):
        return pltpu.make_async_remote_copy(
            ex.at[o, q], ex.at[o, q], send, ex_rs.at[o, q],
            device_id=(me_i, j), device_id_type=MESH,
        )

    def ex_up(o, q):
        return ex_copy(o, q, ex_fw.at[o, q], me_j + CORES)

    def ex_down(o, q):
        return ex_copy(o, q, ex_fw.at[o, q], me_j - CORES)

    def ex_own_down(q):
        return ex_copy(me_j, q, ex_dn.at[q], me_j - CORES)

    def ex_mate(o, q):
        return ex_copy(o, q, ex_pt.at[o, q], mate)

    up_z, down_z = z < line - 1, z > 0

    def send_own(q):
        pl.when(up_z)(lambda: ex_up(me_j, q).start())
        pl.when(down_z)(lambda: ex_own_down(q).start())
        ex_mate(me_j, q).start()

    def relay(d, q):
        below, above = me_j - CORES * d, me_j + CORES * d

        @pl.when(z - d >= 0)
        def _():
            ex_mate(below, q).wait_recv()
            pl.when(up_z)(lambda: ex_up(below, q).start())
            ex_mate(below, q).start()

        @pl.when(z + d < line)
        def _():
            ex_mate(above, q).wait_recv()
            pl.when(down_z)(lambda: ex_down(above, q).start())
            ex_mate(above, q).start()

    w3 = split_weights(w_ref[...])
    lane = lax.broadcasted_iota(jnp.int32, (heads, rows), 1)
    peaks[me_j] = jnp.zeros((heads, rows), jnp.float32)

    def pair_chunk(q, carry):
        pair_in(q).wait()
        top = peaks[me_j]
        for t in range(CHUNK // TILE):
            scores = tile_scores(pair[q, t * TILE : (t + 1) * TILE], w3)
            for k in range(TILE):
                one = scores[:, k * cols : (k + 1) * cols]
                peak = jnp.max(one, axis=1, keepdims=True)
                hold[:, t * TILE + k, :] = jnp.exp(one - peak)
                top = jnp.where(lane == q * CHUNK + t * TILE + k, peak, top)
        peaks[me_j] = top
        ex[me_j, q] = hold[...].astype(jnp.bfloat16)
        send_own(q)
        pl.when(q >= LAG)(lambda: relay(1, q - LAG))
        pl.when(q == chunks - 1)(first_relays)
        return carry

    lax.fori_loop(0, chunks, pair_chunk, 0)

    def peak_copy(o, j):
        return pltpu.make_async_remote_copy(
            peaks.at[o], peaks.at[o], pk_ss.at[j], pk_rs.at[o],
            device_id=(me_i, j), device_id_type=MESH,
        )

    def others(f):
        lax.fori_loop(1, pj_count, lambda r, c: (f((me_j + r) % pj_count), c)[1], 0)

    others(lambda j: peak_copy(me_j, j).start())

    gain = jnp.broadcast_to(gain_ref[...], (chans, 128))
    shift = jnp.broadcast_to(shift_ref[...], (chans, 128))
    gain = jnp.concatenate([gain] * (rows // 128), axis=1)
    shift = jnp.concatenate([shift] * (rows // 128), axis=1)

    def normed(p, s):
        v = msa[p, s].astype(jnp.float32)
        v = v - jnp.mean(v, axis=0, keepdims=True)
        variance = jnp.mean(v * v, axis=0, keepdims=True)
        return (v * lax.rsqrt(variance + EPS) * gain + shift).astype(jnp.bfloat16)

    def gate_group(g, carry):
        for k in range(GROUP):
            s = g * GROUP + k
            gate[s] = jax.nn.sigmoid(dot(ws_ref[...], normed(me_i, s)))
        return carry

    lax.fori_loop(0, seqs // GROUP, gate_group, 0)

    vals[:, span:, :] = jnp.ones((heads, 16, rows), jnp.bfloat16)

    def zero_head(h, carry):
        acc[h] = jnp.zeros(acc.shape[1:], jnp.float32)
        return carry

    lax.fori_loop(0, heads, zero_head, 0)

    others(lambda j: peak_copy(j, me_j).wait_recv())
    scale[...] = jnp.exp(peaks[...] - jnp.max(peaks[...], axis=0, keepdims=True))

    def process(p):
        pl.when(p % 2 != x)(lambda: take(p, 1))

        def value_group(g, carry):
            for k in range(GROUP):
                s = g * GROUP + k
                v = dot(wv_ref[...], normed(p, s)).astype(jnp.bfloat16)
                at = pl.ds(pl.multiple_of(s * width, width), width)
                for h in range(heads):
                    vals[h, at, :] = v[h * width : (h + 1) * width]
            return carry

        lax.fori_loop(0, seqs // GROUP, value_group, 0)

        far = p * CORES + (1 - core)
        lax.fori_loop(0, chunks, lambda q, c: (ex_mate(far, q).wait_recv(), c)[1], 0)
        both = scale[pl.ds(p * CORES, CORES)].reshape(CORES * heads, rows)
        pad = jnp.zeros((128 - CORES * heads, rows), jnp.float32)
        turned = jnp.concatenate([both, pad], axis=0).T
        for c in range(CORES):
            for h in range(heads):
                e = ex[p * CORES + c, :, h].reshape(rows, cols).astype(jnp.float32)
                e = e * turned[:, c * heads + h : c * heads + h + 1]
                weights[h, :, c * cols : (c + 1) * cols] = e.astype(jnp.bfloat16)

        def head(h, carry):
            acc[h] += dot(vals[h], weights[h], NT)
            return carry

        lax.fori_loop(0, heads, head, 0)

    def stage_of(p):
        apart = jnp.where(p > z, p - z, z - p)
        same_row, same_column = p // 2 == y, p % 2 == x
        kind = jnp.where(same_row | same_column, min(2, line - 1), line - 1)
        kind = jnp.where(p == me_i, 1, kind)
        return jnp.where(apart > kind, apart, kind)

    def stage(d, carry):
        first = jnp.where(d == 1, chunks - LAG, 0)
        lax.fori_loop(first, chunks, lambda q, c: (relay(d, q), c)[1], 0)

        @pl.when(d == min(2, line - 1))
        def _():
            for e in range(1, yline):
                pass_y(e, x, 0, False)

        @pl.when(d == line - 1)
        def _():
            for e in range(1, yline):
                pass_y(e, 1 - x, 0, False)

        def block(p, c):
            pl.when(stage_of(p) == d)(lambda: process(p))
            return c

        lax.fori_loop(0, pi_count, block, 0)
        return carry

    lax.fori_loop(1, line, stage, 0)

    inverse = 1.0 / acc[:, span : span + 8, :]
    inverse = inverse[:, :1, :]

    def close_group(g, carry):
        for k in range(GROUP):
            s = g * GROUP + k
            at = pl.ds(pl.multiple_of(s * width, width), width)
            share = gate[s].reshape(heads, width, rows)
            mixed = (share * (acc[:, at, :] * inverse)).astype(jnp.bfloat16)
            out_ref[s] = dot(wc_ref[...], mixed.reshape(heads * width, rows)).astype(jnp.bfloat16)
        return carry

    lax.fori_loop(0, seqs // GROUP, close_group, 0)

    others(lambda j: peak_copy(me_j, j).wait_send())
    for h in range(2):
        to_x(me_i, h).wait_send()
        for p in (me_i, x_near):
            if h == 0:
                pl.when(up_y)(lambda: to_up(p, h).wait_send())
                pl.when(down_y)(lambda: to_down(p, h).wait_send())
    pl.when(up_y)(lambda: to_up(me_i, 1).wait_send())
    pl.when(down_y)(lambda: to_down(me_i, 1).wait_send())
    for e in range(1, yline):
        for column, h, cross in ((x, 1, True), (x, 0, False), (1 - x, 0, False)):
            below, above = me_i - x + column - 2 * e, me_i - x + column + 2 * e

            @pl.when(y - e >= 0)
            def _():
                pl.when(up_y)(lambda: to_up(below, h).wait_send())
                if cross:
                    to_x(below, h).wait_send()

            @pl.when(y + e < yline)
            def _():
                pl.when(down_y)(lambda: to_down(above, h).wait_send())
                if cross:
                    to_x(above, h).wait_send()

    def drain(q, carry):
        pl.when(up_z)(lambda: ex_up(me_j, q).wait_send())
        pl.when(down_z)(lambda: ex_own_down(q).wait_send())
        ex_mate(me_j, q).wait_send()

        def far_sent(d, c):
            below, above = me_j - CORES * d, me_j + CORES * d

            @pl.when(z - d >= 0)
            def _():
                pl.when(up_z)(lambda: ex_up(below, q).wait_send())
                ex_mate(below, q).wait_send()

            @pl.when(z + d < line)
            def _():
                pl.when(down_z)(lambda: ex_down(above, q).wait_send())
                ex_mate(above, q).wait_send()

            return c

        lax.fori_loop(1, line, far_sent, 0)
        return carry

    lax.fori_loop(0, chunks, drain, 0)


def body(pi_count, pj_count, duo, duo_w, aligned, gain, shift, payload_w, switch_w, closing_w):
    rows, cols, pair_chans = duo.shape
    seqs, chans, tokens = aligned.shape
    heads, joint = duo_w.shape[1], payload_w.shape[1]
    span = seqs * (joint // heads)
    chunks = rows // CHUNK
    assert tokens == rows == CORES * cols and pj_count == CORES * pi_count
    vmem = pl.BlockSpec(memory_space=pltpu.VMEM)
    hbm = pl.BlockSpec(memory_space=pl.ANY)
    dma = pltpu.SemaphoreType.DMA
    return pl.pallas_call(
        functools.partial(kernel, pi_count, pj_count),
        in_specs=[hbm, vmem, hbm] + [vmem] * 5,
        out_specs=vmem,
        out_shape=jax.ShapeDtypeStruct(aligned.shape, jnp.bfloat16),
        scratch_shapes=[
            pltpu.VMEM((chunks, CHUNK, cols, pair_chans), jnp.bfloat16),
            pltpu.VMEM((pi_count, seqs, chans, tokens), jnp.bfloat16),
            pltpu.VMEM((pj_count, chunks, heads, CHUNK, cols), jnp.bfloat16),
            pltpu.VMEM((heads, CHUNK, cols), jnp.float32),
            pltpu.VMEM((pj_count, heads, rows), jnp.float32),
            pltpu.VMEM((pj_count, heads, rows), jnp.float32),
            pltpu.VMEM((heads, span + 16, rows), jnp.bfloat16),
            pltpu.VMEM((heads, rows, CORES * cols), jnp.bfloat16),
            pltpu.VMEM((heads, span + 16, rows), jnp.float32),
            pltpu.VMEM((seqs, joint, tokens), jnp.float32),
            dma((chunks,)),
            dma,
            dma((pj_count, chunks)),
            dma((pj_count, chunks)),
            dma((chunks,)),
            dma((pj_count, chunks)),
            dma((pj_count,)),
            dma((pj_count,)),
            dma((pi_count, 2)),
            dma((pi_count, 2)),
            dma((pi_count, 2)),
            dma((pi_count, 2)),
        ],
        compiler_params=pltpu.CompilerParams(
            collective_id=0, has_side_effects=True, vmem_limit_bytes=60 << 20
        ),
        name="layer",
    )(
        duo,
        duo_w.T,
        aligned,
        gain[:, None],
        shift[:, None],
        payload_w.T,
        switch_w.T,
        closing_w.T,
    )


def solution(mesh):
    return jax.shard_map(
        functools.partial(body, mesh.shape["pi"], mesh.shape["pj"]),
        mesh=mesh,
        in_specs=(P("pi", "pj", None), P(), P("pj", None, "pi"), P(), P(), P(), P(), P()),
        out_specs=P("pj", None, "pi"),
        check_vma=False,
    )
```

profile of v0, /device:TPU:4, one launch (start us, length us, event | category | flops | bytes accessed | tf_op | source)
XLA Modules:
  0.0 70.6 jit_solution(813903843464468262)
XLA Ops:
  0.0 1.4 %copy.11.gain_ref = f32[64,1]{1,0:T(8,128)} copy(f32[64,1]{0,1:T(1,128)} %bitcast.10) | data formatting | bytes 512 | tf_op jit(solution)/shard_map/broadcast_in_dim | solution.py:447
  1.4 1.3 %copy.12.shift_ref = f32[64,1]{1,0:T(8,128)} copy(f32[64,1]{0,1:T(1,128)} %bitcast.11) | data formatting | bytes 512 | tf_op jit(solution)/shard_map/broadcast_in_dim | solution.py:448
  2.7 1.5 %copy.9 = bf16[64,256]{0,1:T(8,128)(2,1)} copy(bf16[64,256]{1,0:T(8,128)(2,1)} %param.13) | data formatting | bytes 65536 | tf_op args[5]
  4.2 1.5 %copy.10 = bf16[64,256]{0,1:T(8,128)(2,1)} copy(bf16[64,256]{1,0:T(8,128)(2,1)} %param.14) | data formatting | bytes 65536 | tf_op args[6]
  5.7 62.6 %layer.1 = bf16[32,64,256]{2,1,0:T(8,128)(2,1)} custom-call(bf16[256,128,128]{2,1,0:T(8,128)(2,1)} %pair_hbm.1, f32[8,128]{1,0:T(8,128)} %bitcast.9, bf16[32,64,256]{2,1,0:T(8,128)(2,1)} %msa_hbm.1, f32[64,1]{1,0:T(8,128)} %copy.11.gain_ref, f32[64,1]{1,0:T(8,128)} %copy.12.shift_ref, bf16[256,64]{1,0:T(8,128)(2,1)} %bitcast.6, bf16[256,64]{1,0:T(8,128)(2,1)} %bitcast.7, ...), custom_call_target="tpu_custom_call" | custom-call | tf_op jit(solution)/shard_map/layer/pallas_call | solution.py:410
  68.3 2.3 %copy.14 = bf16[32,64,256]{2,1,0:T(8,128)(2,1)} copy(bf16[32,64,256]{2,1,0:T(8,128)(2,1)} %layer.1) | data formatting | bytes 2097152
where the time goes:
time: 70.9 us; the launch traced here: 70.6 us
  Pallas kernels  62.6 us (88%)
  local copies, waits for them, and re-layouts  7.97 us (11%)
    pallas_call x1, Pallas kernels, body(): pl.pallas_call(functools.partial(kernel, pi_count, pj_count), in_specs=[h...  62.6 us
    unnamed x3, local copies, waits for them, and re-layouts  5.27 us

commit v1 on v0

--- a/solution.py
+++ b/solution.py
@@ -13,8 +13,8 @@
 CORES = 2
 TILE = 16
 CHUNK = 32
-LAG = 3
 GROUP = 8
+HELD = 3
 
 
 def dot(a, b, dims=(((1,), (0,)), ((), ()))):
@@ -53,10 +53,13 @@
     msa_hbm,
     gain_ref,
     shift_ref,
+    payload_ref,
+    switch_ref,
+    wc_ref,
+    out_ref,
     wv_ref,
     ws_ref,
-    wc_ref,
-    out_ref,
+    spread,
     pair,
     msa,
     ex,
@@ -89,7 +92,7 @@
     rows = chunks * CHUNK
     seqs, chans = msa.shape[1], msa.shape[2]
     half = seqs // 2
-    span = vals.shape[1] - 16
+    span = vals.shape[2] - 16
     width = span // seqs
     mate = me_j - core + (1 - core)
     x_near = me_i - x + (1 - x)
@@ -111,107 +114,20 @@
     up_y, down_y = y < yline - 1, y > 0
     pl.when(up_y)(lambda: greet(me_i + 2, me_j))
     pl.when(down_y)(lambda: greet(me_i - 2, me_j))
-    pl.semaphore_wait(barrier, pj_count + jnp.where(up_y, 1, 0) + jnp.where(down_y, 1, 0))
-
-    def part(p, h):
-        return msa.at[p, pl.ds(h * half, half)]
-
-    def msa_copy(p, h, send, i):
-        return pltpu.make_async_remote_copy(
-            part(p, h), part(p, h), send.at[p, h], ms_rs.at[p, h],
-            device_id=(i, me_j), device_id_type=MESH,
-        )
-
-    def to_x(p, h):
-        return msa_copy(p, h, ms_sx, x_near)
-
-    def to_up(p, h):
-        return msa_copy(p, h, ms_up, me_i + 2)
-
-    def to_down(p, h):
-        return msa_copy(p, h, ms_dn, me_i - 2)
-
-    def along_y(p, h):
-        pl.when(up_y)(lambda: to_up(p, h).start())
-        pl.when(down_y)(lambda: to_down(p, h).start())
-
-    def take(p, h):
-        to_x(p, h).wait_recv()
-
-    own_in.wait()
-    to_x(me_i, 0).start()
-    along_y(me_i, 1)
-    to_x(me_i, 1).start()
-    along_y(me_i, 0)
-
-    def pass_y(e, column, h, cross):
-        below, above = me_i - x + column - 2 * e, me_i - x + column + 2 * e
-
-        @pl.when(y - e >= 0)
-        def _():
-            take(below, h)
-            pl.when(up_y)(lambda: to_up(below, h).start())
-            if cross:
-                to_x(below, h).start()
-
-        @pl.when(y + e < yline)
-        def _():
-            take(above, h)
-            pl.when(down_y)(lambda: to_down(above, h).start())
-            if cross:
-                to_x(above, h).start()
-
-    def first_relays():
-        take(x_near, 0)
-        along_y(x_near, 0)
-        for e in range(1, yline):
-            pass_y(e, x, 1, True)
-
-    def ex_copy(o, q, send, j):
-        return pltpu.make_async_remote_copy(
-            ex.at[o, q], ex.at[o, q], send, ex_rs.at[o, q],
-            device_id=(me_i, j), device_id_type=MESH,
-        )
-
-    def ex_up(o, q):
-        return ex_copy(o, q, ex_fw.at[o, q], me_j + CORES)
-
-    def ex_down(o, q):
-        return ex_copy(o, q, ex_fw.at[o, q], me_j - CORES)
-
-    def ex_own_down(q):
-        return ex_copy(me_j, q, ex_dn.at[q], me_j - CORES)
-
-    def ex_mate(o, q):
-        return ex_copy(o, q, ex_pt.at[o, q], mate)
-
-    up_z, down_z = z < line - 1, z > 0
-
-    def send_own(q):
-        pl.when(up_z)(lambda: ex_up(me_j, q).start())
-        pl.when(down_z)(lambda: ex_own_down(q).start())
-        ex_mate(me_j, q).start()
-
-    def relay(d, q):
-        below, above = me_j - CORES * d, me_j + CORES * d
-
-        @pl.when(z - d >= 0)
-        def _():
-            ex_mate(below, q).wait_recv()
-            pl.when(up_z)(lambda: ex_up(below, q).start())
-            ex_mate(below, q).start()
-
-        @pl.when(z + d < line)
-        def _():
-            ex_mate(above, q).wait_recv()
-            pl.when(down_z)(lambda: ex_down(above, q).start())
-            ex_mate(above, q).start()
+
+    wv_ref[...] = payload_ref[...].astype(jnp.float32).T.astype(jnp.bfloat16)
+    ws_ref[...] = switch_ref[...].astype(jnp.float32).T.astype(jnp.bfloat16)
+    diagonal = lax.broadcasted_iota(jnp.int32, (chans, chans), 0)
+    diagonal = diagonal == lax.broadcasted_iota(jnp.int32, (chans, chans), 1)
+    for k, ref in enumerate((gain_ref, shift_ref)):
+        column = jnp.sum(jnp.where(diagonal, ref[...], 0.0), axis=1, keepdims=True)
+        spread[k] = jnp.broadcast_to(column, (chans, rows))
 
     w3 = split_weights(w_ref[...])
     lane = lax.broadcasted_iota(jnp.int32, (heads, rows), 1)
     peaks[me_j] = jnp.zeros((heads, rows), jnp.float32)
 
-    def pair_chunk(q, carry):
+    def pair_chunk(q):
         pair_in(q).wait()
         top = peaks[me_j]
         for t in range(CHUNK // TILE):
@@ -223,12 +139,104 @@
                 top = jnp.where(lane == q * CHUNK + t * TILE + k, peak, top)
         peaks[me_j] = top
         ex[me_j, q] = hold[...].astype(jnp.bfloat16)
-        send_own(q)
-        pl.when(q >= LAG)(lambda: relay(1, q - LAG))
-        pl.when(q == chunks - 1)(first_relays)
-        return carry
-
-    lax.fori_loop(0, chunks, pair_chunk, 0)
+
+    pair_chunk(0)
+
+    pl.semaphore_wait(barrier, pj_count + jnp.where(up_y, 1, 0) + jnp.where(down_y, 1, 0))
+
+    def part(p, h):
+        return msa.at[p, pl.ds(h * half, half)]
+
+    def msa_copy(p, h, send, i):
+        return pltpu.make_async_remote_copy(
+            part(p, h), part(p, h), send.at[p, h], ms_rs.at[p, h],
+            device_id=(i, me_j), device_id_type=MESH,
+        )
+
+    def to_x(p, h):
+        return msa_copy(p, h, ms_sx, x_near)
+
+    def to_up(p, h):
+        return msa_copy(p, h, ms_up, me_i + 2)
+
+    def to_down(p, h):
+        return msa_copy(p, h, ms_dn, me_i - 2)
+
+    def along_y(p, h):
+        pl.when(up_y)(lambda: to_up(p, h).start())
+        pl.when(down_y)(lambda: to_down(p, h).start())
+
+    def take(p, h):
+        to_x(p, h).wait_recv()
+
+    own_in.wait()
+    to_x(me_i, 0).start()
+    along_y(me_i, 1)
+    to_x(me_i, 1).start()
+    along_y(me_i, 0)
+
+    def pass_y(e, column, h, cross):
+        below, above = me_i - x + column - 2 * e, me_i - x + column + 2 * e
+
+        @pl.when(y - e >= 0)
+        def _():
+            take(below, h)
+            pl.when(up_y)(lambda: to_up(below, h).start())
+            if cross:
+                to_x(below, h).start()
+
+        @pl.when(y + e < yline)
+        def _():
+            take(above, h)
+            pl.when(down_y)(lambda: to_down(above, h).start())
+            if cross:
+                to_x(above, h).start()
+
+    def first_relays():
+        take(x_near, 0)
+        along_y(x_near, 0)
+        for e in range(1, yline):
+            pass_y(e, x, 1, True)
+
+    def ex_copy(o, q, send, j):
+        return pltpu.make_async_remote_copy(
+            ex.at[o, q], ex.at[o, q], send, ex_rs.at[o, q],
+            device_id=(me_i, j), device_id_type=MESH,
+        )
+
+    def ex_up(o, q):
+        return ex_copy(o, q, ex_fw.at[o, q], me_j + CORES)
+
+    def ex_down(o, q):
+        return ex_copy(o, q, ex_fw.at[o, q], me_j - CORES)
+
+    def ex_own_down(q):
+        return ex_copy(me_j, q, ex_dn.at[q], me_j - CORES)
+
+    def ex_mate(o, q):
+        return ex_copy(o, q, ex_pt.at[o, q], mate)
+
+    up_z, down_z = z < line - 1, z > 0
+
+    def send_own(q):
+        pl.when(up_z)(lambda: ex_up(me_j, q).start())
+        pl.when(down_z)(lambda: ex_own_down(q).start())
+        ex_mate(me_j, q).start()
+
+    def relay(d, q):
+        below, above = me_j - CORES * d, me_j + CORES * d
+
+        @pl.when(z - d >= 0)
+        def _():
+            ex_mate(below, q).wait_recv()
+            pl.when(up_z)(lambda: ex_up(below, q).start())
+            ex_mate(below, q).start()
+
+        @pl.when(z + d < line)
+        def _():
+            ex_mate(above, q).wait_recv()
+            pl.when(down_z)(lambda: ex_down(above, q).start())
+            ex_mate(above, q).start()
 
     def peak_copy(o, j):
         return pltpu.make_async_remote_copy(
@@ -239,18 +247,18 @@
     def others(f):
         lax.fori_loop(1, pj_count, lambda r, c: (f((me_j + r) % pj_count), c)[1], 0)
 
+    send_own(0)
+    lax.fori_loop(1, chunks, lambda q, c: (pair_chunk(q), send_own(q), c)[2], 0)
     others(lambda j: peak_copy(me_j, j).start())
 
-    gain = jnp.broadcast_to(gain_ref[...], (chans, 128))
-    shift = jnp.broadcast_to(shift_ref[...], (chans, 128))
-    gain = jnp.concatenate([gain] * (rows // 128), axis=1)
-    shift = jnp.concatenate([shift] * (rows // 128), axis=1)
+    def relays(d, first, last):
+        lax.fori_loop(first, last, lambda q, c: (relay(d, q), c)[1], 0)
 
     def normed(p, s):
         v = msa[p, s].astype(jnp.float32)
         v = v - jnp.mean(v, axis=0, keepdims=True)
         variance = jnp.mean(v * v, axis=0, keepdims=True)
-        return (v * lax.rsqrt(variance + EPS) * gain + shift).astype(jnp.bfloat16)
+        return (v * lax.rsqrt(variance + EPS) * spread[0] + spread[1]).astype(jnp.bfloat16)
 
     def gate_group(g, carry):
         for k in range(GROUP):
@@ -258,9 +266,13 @@
             gate[s] = jax.nn.sigmoid(dot(ws_ref[...], normed(me_i, s)))
         return carry
 
+    relays(1, 0, chunks - 2)
     lax.fori_loop(0, seqs // GROUP, gate_group, 0)
-
-    vals[:, span:, :] = jnp.ones((heads, 16, rows), jnp.bfloat16)
+    relays(1, chunks - 2, chunks)
+    first_relays()
+
+    for slot in range(2):
+        vals[slot, :, span:, :] = jnp.ones((heads, 16, rows), jnp.bfloat16)
 
     def zero_head(h, carry):
         acc[h] = jnp.zeros(acc.shape[1:], jnp.float32)
@@ -271,7 +283,7 @@
     others(lambda j: peak_copy(j, me_j).wait_recv())
     scale[...] = jnp.exp(peaks[...] - jnp.max(peaks[...], axis=0, keepdims=True))
 
-    def process(p):
+    def values(p, slot):
         pl.when(p % 2 != x)(lambda: take(p, 1))
 
         def value_group(g, carry):
@@ -280,57 +292,76 @@
                 v = dot(wv_ref[...], normed(p, s)).astype(jnp.bfloat16)
                 at = pl.ds(pl.multiple_of(s * width, width), width)
                 for h in range(heads):
-                    vals[h, at, :] = v[h * width : (h + 1) * width]
+                    vals[slot, h, at, :] = v[h * width : (h + 1) * width]
             return carry
 
         lax.fori_loop(0, seqs // GROUP, value_group, 0)
 
+    def attend(p, slot):
         far = p * CORES + (1 - core)
         lax.fori_loop(0, chunks, lambda q, c: (ex_mate(far, q).wait_recv(), c)[1], 0)
         both = scale[pl.ds(p * CORES, CORES)].reshape(CORES * heads, rows)
         pad = jnp.zeros((128 - CORES * heads, rows), jnp.float32)
         turned = jnp.concatenate([both, pad], axis=0).T
-        for c in range(CORES):
-            for h in range(heads):
+        for h in range(heads):
+            for c in range(CORES):
                 e = ex[p * CORES + c, :, h].reshape(rows, cols).astype(jnp.float32)
                 e = e * turned[:, c * heads + h : c * heads + h + 1]
                 weights[h, :, c * cols : (c + 1) * cols] = e.astype(jnp.bfloat16)
-
-        def head(h, carry):
-            acc[h] += dot(vals[h], weights[h], NT)
-            return carry
-
-        lax.fori_loop(0, heads, head, 0)
-
-    def stage_of(p):
-        apart = jnp.where(p > z, p - z, z - p)
-        same_row, same_column = p // 2 == y, p % 2 == x
-        kind = jnp.where(same_row | same_column, min(2, line - 1), line - 1)
-        kind = jnp.where(p == me_i, 1, kind)
-        return jnp.where(apart > kind, apart, kind)
-
-    def stage(d, carry):
-        first = jnp.where(d == 1, chunks - LAG, 0)
-        lax.fori_loop(first, chunks, lambda q, c: (relay(d, q), c)[1], 0)
-
-        @pl.when(d == min(2, line - 1))
+        for h in range(heads):
+            acc[h] += dot(vals[slot, h], weights[h], NT)
+
+    def apart(p):
+        return jnp.where(p > z, p - z, z - p)
+
+    def crosses(p):
+        return (p // 2 != y) & (p % 2 != x)
+
+    def attend_unit(p):
+        near = jnp.where(apart(p) <= 1, jnp.where(p == me_i, 0, 1), apart(p))
+        unit = jnp.where(crosses(p), line - 1, near)
+        return jnp.where(apart(p) == line - 1, line, unit)
+
+    def value_unit(p):
+        early = jnp.where(crosses(p), line - 1, line - 2)
+        return jnp.where(apart(p) == line - 1, early, attend_unit(p))
+
+    half_way = chunks // 2
+
+    def step(n, carry):
+        u, p = n // pi_count, n % pi_count
+        fresh = p == 0
+
+        @pl.when(fresh & (u == 1))
         def _():
             for e in range(1, yline):
                 pass_y(e, x, 0, False)
-
-        @pl.when(d == line - 1)
-        def _():
+            relays(2, 0, half_way)
+
+        @pl.when((u == 1) & (p < chunks - half_way))
+        def _():
+            relay(2, half_way + p)
+
+        @pl.when(fresh & (u >= 3) & (u < line - 1))
+        def _():
+            relays(u, 0, chunks)
+
+        @pl.when(fresh & (u == line - 1))
+        def _():
+            relays(line - 1, 0, chunks - HELD)
             for e in range(1, yline):
                 pass_y(e, 1 - x, 0, False)
 
-        def block(p, c):
-            pl.when(stage_of(p) == d)(lambda: process(p))
-            return c
-
-        lax.fori_loop(0, pi_count, block, 0)
+        @pl.when(fresh & (u == line))
+        def _():
+            relays(line - 1, chunks - HELD, chunks)
+
+        slot = jnp.where(apart(p) == line - 1, 1, 0)
+        pl.when(value_unit(p) == u)(lambda: values(p, slot))
+        pl.when(attend_unit(p) == u)(lambda: attend(p, slot))
         return carry
 
-    lax.fori_loop(1, line, stage, 0)
+    lax.fori_loop(0, (line + 1) * pi_count, step, 0)
 
     inverse = 1.0 / acc[:, span : span + 8, :]
     inverse = inverse[:, :1, :]
@@ -404,6 +435,7 @@
     span = seqs * (joint // heads)
     chunks = rows // CHUNK
     assert tokens == rows == CORES * cols and pj_count == CORES * pi_count
+    assert pi_count >= 4 and pi_count >= chunks // 2
     vmem = pl.BlockSpec(memory_space=pltpu.VMEM)
     hbm = pl.BlockSpec(memory_space=pl.ANY)
     dma = pltpu.SemaphoreType.DMA
@@ -413,13 +445,16 @@
         out_specs=vmem,
         out_shape=jax.ShapeDtypeStruct(aligned.shape, jnp.bfloat16),
         scratch_shapes=[
+            pltpu.VMEM((joint, chans), jnp.bfloat16),
+            pltpu.VMEM((joint, chans), jnp.bfloat16),
+            pltpu.VMEM((2, chans, rows), jnp.float32),
             pltpu.VMEM((chunks, CHUNK, cols, pair_chans), jnp.bfloat16),
             pltpu.VMEM((pi_count, seqs, chans, tokens), jnp.bfloat16),
             pltpu.VMEM((pj_count, chunks, heads, CHUNK, cols), jnp.bfloat16),
             pltpu.VMEM((heads, CHUNK, cols), jnp.float32),
             pltpu.VMEM((pj_count, heads, rows), jnp.float32),
             pltpu.VMEM((pj_count, heads, rows), jnp.float32),
-            pltpu.VMEM((heads, span + 16, rows), jnp.bfloat16),
+            pltpu.VMEM((2, heads, span + 16, rows), jnp.bfloat16),
             pltpu.VMEM((heads, rows, CORES * cols), jnp.bfloat16),
             pltpu.VMEM((heads, span + 16, rows), jnp.float32),
             pltpu.VMEM((seqs, joint, tokens), jnp.float32),
@@ -437,17 +472,17 @@
             dma((pi_count, 2)),
         ],
         compiler_params=pltpu.CompilerParams(
-            collective_id=0, has_side_effects=True, vmem_limit_bytes=60 << 20
+            collective_id=0, has_side_effects=True, vmem_limit_bytes=58 << 20
         ),
         name="layer",
     )(
         duo,
         duo_w.T,
         aligned,
-        gain[:, None],
-        shift[:, None],
-        payload_w.T,
-        switch_w.T,
+        gain[None, :],
+        shift[None, :],
+        payload_w,
+        switch_w,
         closing_w.T,
     )
 

time: 70.9 us -> 56.3 us (0.79)
  the two profiles are of different devices: /device:TPU:4 before, /device:TPU:27 now
where the time goes in v1:
time: 56.3 us; the launch traced here: 56 us
  Pallas kernels  53.7 us (95%)
  local copies, waits for them, and re-layouts  2.3 us (4%)
    pallas_call x1, Pallas kernels, body(): pl.pallas_call(functools.partial(kernel, pi_count, pj_count), in_specs=[h...  53.7 us
    unnamed x1, local copies, waits for them, and re-layouts  2.3 us

profile of v1, /device:TPU:27, one launch (start us, length us, event | category | flops | bytes accessed | tf_op | source)
XLA Modules:
  0.0 56.0 jit_solution(8336244490488547564)
XLA Ops:
  0.0 53.7 %layer.1 = bf16[32,64,256]{2,1,0:T(8,128)(2,1)} custom-call(bf16[256,128,128]{2,1,0:T(8,128)(2,1)} %pair_hbm.1, f32[8,128]{1,0:T(8,128)} %bitcast.5, bf16[32,64,256]{2,1,0:T(8,128)(2,1)} %msa_hbm.1, f32[1,64]{1,0:T(1,128)} %bitcast.6, f32[1,64]{1,0:T(1,128)} %bitcast.7, bf16[64,256]{1,0:T(8,128)(2,1)} %payload_ref.1, bf16[64,256]{1,0:T(8,128)(2,1)} %switch_ref.1, ...), custom_call_target="tpu_custom_call" | custom-call | tf_op jit(solution)/shard_map/layer/pallas_call | solution.py:442
  53.7 2.3 %copy.10 = bf16[32,64,256]{2,1,0:T(8,128)(2,1)} copy(bf16[32,64,256]{2,1,0:T(8,128)(2,1)} %layer.1) | data formatting | bytes 2097152

commit v2 on v0

v2 whole, which is shorter than its diff:
```python
import functools

import jax
import jax.numpy as jnp
from jax import lax
from jax.experimental import pallas as pl
from jax.experimental.pallas import tpu as pltpu
from jax.sharding import PartitionSpec as P

EPS = 1e-05
MESH = pl.DeviceIdType.MESH
NT = (((1,), (1,)), ((), ()))
CORES = 2
TILE = 16
CHUNK = 32
GROUP = 16
HELD = 3
VMEM_LIMIT = 58 << 20


def dot(a, b, dims=(((1,), (0,)), ((), ()))):
    return lax.dot_general(a, b, dims, preferred_element_type=jnp.float32)


def split_weights(w):
    w = w - jnp.mean(w, axis=1, keepdims=True)
    hi = w.astype(jnp.bfloat16).astype(jnp.float32)
    mid = (w - hi).astype(jnp.bfloat16).astype(jnp.float32)
    w3 = jnp.concatenate([hi, mid, w - hi - mid, jnp.zeros_like(w)], axis=0)
    return w3.astype(jnp.bfloat16)


def tile_scores(x, w3):
    rows, cols, chans = x.shape
    heads = w3.shape[0] // 4
    x = x.reshape(rows * cols, chans)
    mean = dot(x, jnp.ones((chans, chans), jnp.bfloat16)) * (1.0 / chans)
    centred = x.astype(jnp.float32) - mean
    square = centred * centred
    top = square.astype(jnp.bfloat16)
    rest = (square - top.astype(jnp.float32)).astype(jnp.bfloat16)
    ones = jnp.ones((2 * heads, 2 * chans), jnp.bfloat16)
    variance = dot(ones, jnp.concatenate([top, rest], axis=1), NT)[:heads] * (1.0 / chans)
    parts = dot(w3, x, NT)
    scores = parts[:heads] + (parts[heads : 2 * heads] + parts[2 * heads : 3 * heads])
    return scores * lax.rsqrt(variance + EPS)


def kernel(
    pi_count,
    pj_count,
    pair_hbm,
    w_ref,
    msa_hbm,
    gain_ref,
    shift_ref,
    payload_ref,
    switch_ref,
    wc_ref,
    out_ref,
    wv_ref,
    ws_ref,
    spread,
    pair,
    msa,
    ex,
    hold,
    peaks,
    scale,
    vals,
    weights,
    acc,
    gate,
    pair_sem,
    msa_sem,
    ex_rs,
    ex_fw,
    ex_dn,
    ex_pt,
    ex_far,
    pk_rs,
    pk_ss,
    ms_rs,
    ms_sx,
    ms_up,
    ms_dn,
):
    me_i, me_j = lax.axis_index("pi"), lax.axis_index("pj")
    line, yline = pj_count // CORES, pi_count // 2
    z, core = me_j // CORES, me_j % CORES
    y, x = me_i // 2, me_i % 2
    chunks = ex.shape[1]
    heads, cols = ex.shape[2], ex.shape[4]
    rows = chunks * CHUNK
    seqs, half, chans = out_ref.shape[0], msa.shape[1], msa.shape[2]
    span = vals.shape[2] - 16
    width = span // seqs
    mate = me_j - core + (1 - core)
    x_near = me_i - x + (1 - x)

    pair_in = lambda q: pltpu.make_async_copy(
        pair_hbm.at[pl.ds(q * CHUNK, CHUNK)], pair.at[q], pair_sem.at[q]
    )
    own_in = [
        pltpu.make_async_copy(msa_hbm.at[pl.ds(h * half, half)], msa.at[me_i * 2 + h], msa_sem.at[h])
        for h in range(2)
    ]
    for h in range(2):
        own_in[h].start()
    lax.fori_loop(0, chunks, lambda q, c: (pair_in(q).start(), c)[1], 0)

    barrier = pltpu.get_barrier_semaphore()

    def greet(i, j):
        pl.semaphore_signal(barrier, inc=1, device_id=(i, j), device_id_type=MESH)

    lax.fori_loop(1, pj_count, lambda r, c: (greet(me_i, (me_j + r) % pj_count), c)[1], 0)
    greet(x_near, me_j)
    up_y, down_y = y < yline - 1, y > 0
    pl.when(up_y)(lambda: greet(me_i + 2, me_j))
    pl.when(down_y)(lambda: greet(me_i - 2, me_j))

    pl.semaphore_wait(barrier, pj_count + jnp.where(up_y, 1, 0) + jnp.where(down_y, 1, 0))

    def msa_copy(p, h, send, i, count=1):
        part = msa.at[pl.ds(p * 2 + h, count)]
        return pltpu.make_async_remote_copy(
            part, part, send, ms_rs.at[p, h], device_id=(i, me_j), device_id_type=MESH
        )

    def to_x(p, h):
        return msa_copy(p, h, ms_sx, x_near)

    def to_up(p, h, e):
        return msa_copy(p, h, ms_up.at[e], me_i + 2)

    def to_down(p, h, e):
        return msa_copy(p, h, ms_dn.at[e], me_i - 2)

    def along_y(p, h):
        pl.when(up_y)(lambda: to_up(p, h, 0).start())
        pl.when(down_y)(lambda: to_down(p, h, 0).start())

    def take(p, h):
        to_x(p, h).wait_recv()

    for h in range(2):
        own_in[h].wait()
    to_x(me_i, 0).start()
    along_y(me_i, 1)
    to_x(me_i, 1).start()
    along_y(me_i, 0)

    def pass_y(e, column, h, cross):
        below, above = me_i - x + column - 2 * e, me_i - x + column + 2 * e

        @pl.when(y - e >= 0)
        def _():
            take(below, h)
            pl.when(up_y)(lambda: to_up(below, h, e).start())
            if cross:
                to_x(below, h).start()

        @pl.when(y + e < yline)
        def _():
            take(above, h)
            pl.when(down_y)(lambda: to_down(above, h, e).start())
            if cross:
                to_x(above, h).start()

    def first_relays():
        take(x_near, 0)
        along_y(x_near, 0)
        for e in range(1, yline):
            pass_y(e, x, 1, True)

    def ex_copy(o, q, send, receive, j):
        block = ex.at[o] if q is None else ex.at[o, q]
        return pltpu.make_async_remote_copy(
            block, block, send, receive, device_id=(me_i, j), device_id_type=MESH
        )

    def ex_along(o, q, send, j):
        c = o // CORES
        return ex_copy(o, q, send, ex_rs.at[c, 0 if q is None else q], j)

    def ex_up(o, q=None):
        return ex_along(o, q, ex_fw.at[o // CORES], me_j + CORES)

    def ex_down(o, q=None):
        return ex_along(o, q, ex_fw.at[o // CORES], me_j - CORES)

    def ex_own_down(q=None):
        return ex_along(me_j, q, ex_dn, me_j - CORES)

    def ex_mate(o, q=None):
        return ex_copy(o, q, ex_pt.at[o // CORES], ex_far.at[o // CORES], mate)

    up_z, down_z = z < line - 1, z > 0

    def send_own(q):
        pl.when(up_z)(lambda: ex_up(me_j, q).start())
        pl.when(down_z)(lambda: ex_own_down(q).start())
        ex_mate(me_j, q).start()

    def relay(d, q):
        below, above = me_j - CORES * d, me_j + CORES * d

        @pl.when(z - d >= 0)
        def _():
            ex_up(below, q).wait_recv()
            pl.when(up_z)(lambda: ex_up(below, q).start())
            ex_mate(below, q).start()

        @pl.when(z + d < line)
        def _():
            ex_up(above, q).wait_recv()
            pl.when(down_z)(lambda: ex_down(above, q).start())
            ex_mate(above, q).start()

    def peak_copy(o, j):
        return pltpu.make_async_remote_copy(
            peaks.at[o], peaks.at[o], pk_ss, pk_rs,
            device_id=(me_i, j), device_id_type=MESH,
        )

    def all_peaks():
        part = peaks.at[pl.ds(0, pj_count - 1)]
        return pltpu.make_async_remote_copy(
            part, part, pk_ss, pk_rs, device_id=(me_i, mate), device_id_type=MESH
        )

    def others(f):
        lax.fori_loop(1, pj_count, lambda r, c: (f((me_j + r) % pj_count), c)[1], 0)

    w3 = split_weights(w_ref[...])
    lane = lax.broadcasted_iota(jnp.int32, (heads, rows), 1)
    peaks[me_j] = jnp.zeros((heads, rows), jnp.float32)

    def pair_chunk(q):
        pair_in(q).wait()
        top = peaks[me_j]
        for t in range(CHUNK // TILE):
            scores = tile_scores(pair[q, t * TILE : (t + 1) * TILE], w3)
            for k in range(TILE):
                one = scores[:, k * cols : (k + 1) * cols]
                peak = jnp.max(one, axis=1, keepdims=True)
                hold[:, t * TILE + k, :] = jnp.exp(one - peak)
                top = jnp.where(lane == q * CHUNK + t * TILE + k, peak, top)
        peaks[me_j] = top
        ex[me_j, q] = hold[...].astype(jnp.bfloat16)

    lax.fori_loop(0, chunks, lambda q, c: (pair_chunk(q), send_own(q), c)[2], 0)
    others(lambda j: peak_copy(me_j, j).start())

    def relays(d, first, last):
        lax.fori_loop(first, last, lambda q, c: (relay(d, q), c)[1], 0)

    def normed(p, s):
        v = msa[p * 2 + s // half, s % half].astype(jnp.float32)
        v = v - jnp.mean(v, axis=0, keepdims=True)
        variance = jnp.mean(v * v, axis=0, keepdims=True)
        return (v * lax.rsqrt(variance + EPS) * spread[0] + spread[1]).astype(jnp.bfloat16)

    def gate_group(g, carry):
        for k in range(GROUP):
            s = g * GROUP + k
            gate[s] = jax.nn.sigmoid(dot(ws_ref[...], normed(me_i, s)))
        return carry

    wv_ref[...] = payload_ref[...].astype(jnp.float32).T.astype(jnp.bfloat16)
    ws_ref[...] = switch_ref[...].astype(jnp.float32).T.astype(jnp.bfloat16)
    diagonal = lax.broadcasted_iota(jnp.int32, (chans, chans), 0)
    diagonal = diagonal == lax.broadcasted_iota(jnp.int32, (chans, chans), 1)
    for k, ref in enumerate((gain_ref, shift_ref)):
        column = jnp.sum(jnp.where(diagonal, ref[...], 0.0), axis=1, keepdims=True)
        spread[k] = jnp.broadcast_to(column, (chans, rows))

    relays(1, 0, chunks - 2)
    lax.fori_loop(0, seqs // GROUP, gate_group, 0)
    relays(1, chunks - 2, chunks)
    first_relays()

    for slot in range(2):
        vals[slot, :, span:, :] = jnp.ones((heads, 16, rows), jnp.bfloat16)

    def zero_head(h, carry):
        acc[h] = jnp.zeros(acc.shape[1:], jnp.float32)
        return carry

    lax.fori_loop(0, heads, zero_head, 0)

    all_peaks().wait_recv()
    scale[...] = jnp.exp(peaks[...] - jnp.max(peaks[...], axis=0, keepdims=True))

    def values(p, slot):
        pl.when(p % 2 != x)(lambda: take(p, 1))

        def value_group(g, carry):
            for k in range(GROUP):
                s = g * GROUP + k
                v = dot(wv_ref[...], normed(p, s)).astype(jnp.bfloat16)
                at = pl.ds(pl.multiple_of(s * width, width), width)
                for h in range(heads):
                    vals[slot, h, at, :] = v[h * width : (h + 1) * width]
            return carry

        lax.fori_loop(0, seqs // GROUP, value_group, 0)

    def rescale(p, slot):
        ex_mate(p * CORES + (1 - core)).wait_recv()
        both = scale[pl.ds(p * CORES, CORES)].reshape(CORES * heads, rows)
        pad = jnp.zeros((128 - CORES * heads, rows), jnp.float32)
        turned = jnp.concatenate([both, pad], axis=0).T
        for h in range(heads):
            for c in range(CORES):
                e = ex[p * CORES + c, :, h].reshape(rows, cols).astype(jnp.float32)
                e = e * turned[:, c * heads + h : c * heads + h + 1]
                weights[slot, h, :, c * cols : (c + 1) * cols] = e.astype(jnp.bfloat16)

    def attend(slot, weight_slot):
        for h in range(heads):
            acc[h] += dot(vals[slot, h], weights[weight_slot, h], NT)

    def apart(p):
        return jnp.where(p > z, p - z, z - p)

    def crosses(p):
        return (p // 2 != y) & (p % 2 != x)

    def attend_unit(p):
        near = jnp.where(apart(p) <= 1, jnp.where(p == me_i, 0, 1), apart(p))
        unit = jnp.where(crosses(p), line - 1, near)
        return jnp.where(apart(p) == line - 1, line, unit)

    def value_unit(p):
        early = jnp.where(crosses(p), line - 1, line - 2)
        return jnp.where(apart(p) == line - 1, early, attend_unit(p))

    half_way = chunks // 2
    diagonal_block = (y + 1) % yline * 2 + (1 - x)

    def step(n, carry):
        u, p = n // pi_count, n % pi_count
        fresh = p == 0

        @pl.when(fresh & (u == 1))
        def _():
            relays(2, 0, half_way)
            for e in range(1, yline):
                pass_y(e, x, 0, False)

        @pl.when((u == 1) & (p < chunks - half_way))
        def _():
            relay(2, half_way + p)

        @pl.when(fresh & (u >= 3) & (u < line - 1))
        def _():
            relays(u, 0, chunks)

        @pl.when(fresh & (u == line - 1))
        def _():
            relays(line - 1, 0, chunks - HELD)
            for e in range(1, yline):
                pass_y(e, 1 - x, 0, False)

        @pl.when(fresh & (u == line))
        def _():
            relays(line - 1, chunks - HELD, chunks)

        slot = jnp.where(apart(p) == line - 1, 1, 0)
        early = (p == diagonal_block) & (slot == 0)
        weight_slot = jnp.where(early, 2, slot)
        rescale_unit = jnp.where(early, line - 2, attend_unit(p))
        pl.when(value_unit(p) == u)(lambda: values(p, slot))
        pl.when(rescale_unit == u)(lambda: rescale(p, weight_slot))
        pl.when(attend_unit(p) == u)(lambda: attend(slot, weight_slot))
        return carry

    lax.fori_loop(0, (line + 1) * pi_count, step, 0)

    inverse = 1.0 / acc[:, span : span + 8, :]
    inverse = inverse[:, :1, :]

    def close_group(g, carry):
        for k in range(GROUP):
            s = g * GROUP + k
            at = pl.ds(pl.multiple_of(s * width, width), width)
            share = gate[s].reshape(heads, width, rows)
            mixed = (share * (acc[:, at, :] * inverse)).astype(jnp.bfloat16)
            out_ref[s] = dot(wc_ref[...], mixed.reshape(heads * width, rows)).astype(jnp.bfloat16)
        return carry

    lax.fori_loop(0, seqs // GROUP, close_group, 0)

    all_peaks().wait_send()
    msa_copy(0, 0, ms_sx, x_near, yline + 1).wait_send()
    for e in range(yline):
        pl.when(up_y & (y - e >= 0))(
            lambda: msa_copy(0, 0, ms_up.at[e], me_i + 2, 3).wait_send()
        )
        pl.when(down_y & (y + e < yline))(
            lambda: msa_copy(0, 0, ms_dn.at[e], me_i - 2, 3).wait_send()
        )
    pl.when(down_z)(lambda: ex_own_down().wait_send())

    def drain(c, carry):
        o = c * CORES + core
        ex_mate(o).wait_send()
        pl.when((c <= z) & up_z)(lambda: ex_up(o).wait_send())
        pl.when((c > z) & down_z)(lambda: ex_down(o).wait_send())
        return carry

    lax.fori_loop(0, line, drain, 0)


def body(pi_count, pj_count, duo, duo_w, aligned, gain, shift, payload_w, switch_w, closing_w):
    rows, cols, pair_chans = duo.shape
    seqs, chans, tokens = aligned.shape
    heads, joint = duo_w.shape[1], payload_w.shape[1]
    span = seqs * (joint // heads)
    chunks = rows // CHUNK
    assert tokens == rows == CORES * cols and pj_count == CORES * pi_count
    assert pi_count >= 4 and pi_count >= chunks // 2
    vmem = pl.BlockSpec(memory_space=pltpu.VMEM)
    hbm = pl.BlockSpec(memory_space=pltpu.HBM)
    dma = pltpu.SemaphoreType.DMA
    return pl.pallas_call(
        functools.partial(kernel, pi_count, pj_count),
        in_specs=[hbm, vmem, hbm] + [vmem] * 5,
        out_specs=vmem,
        out_shape=pltpu.VMEM(aligned.shape, jnp.bfloat16),
        scratch_shapes=[
            pltpu.VMEM((joint, chans), jnp.bfloat16),
            pltpu.VMEM((joint, chans), jnp.bfloat16),
            pltpu.VMEM((2, chans, rows), jnp.float32),
            pltpu.VMEM((chunks, CHUNK, cols, pair_chans), jnp.bfloat16),
            pltpu.VMEM((pi_count * 2, seqs // 2, chans, tokens), jnp.bfloat16),
            pltpu.VMEM((pj_count, chunks, heads, CHUNK, cols), jnp.bfloat16),
            pltpu.VMEM((heads, CHUNK, cols), jnp.float32),
            pltpu.VMEM((pj_count, heads, rows), jnp.float32),
            pltpu.VMEM((pj_count, heads, rows), jnp.float32),
            pltpu.VMEM((2, heads, span + 16, rows), jnp.bfloat16),
            pltpu.VMEM((3, heads, rows, CORES * cols), jnp.bfloat16),
            pltpu.VMEM((heads, span + 16, rows), jnp.float32),
            pltpu.VMEM((seqs, joint, tokens), jnp.float32),
            dma((chunks,)),
            dma((2,)),
            dma((pj_count // CORES, chunks)),
            dma((pj_count // CORES,)),
            dma,
            dma((pj_count // CORES,)),
            dma((pj_count // CORES,)),
            dma,
            dma,
            dma((pi_count, 2)),
            dma,
            dma((pi_count // 2,)),
            dma((pi_count // 2,)),
        ],
        compiler_params=pltpu.CompilerParams(
            collective_id=0, has_side_effects=True, vmem_limit_bytes=VMEM_LIMIT
        ),
        name="layer",
    )(
        duo,
        duo_w.T,
        aligned,
        gain[None, :],
        shift[None, :],
        payload_w,
        switch_w,
        closing_w.T,
    )


def solution(mesh):
    return jax.shard_map(
        functools.partial(body, mesh.shape["pi"], mesh.shape["pj"]),
        mesh=mesh,
        in_specs=(P("pi", "pj", None), P(), P("pj", None, "pi"), P(), P(), P(), P(), P()),
        out_specs=P("pj", None, "pi"),
        check_vma=False,
    )
```

time: 70.9 us -> 50.9 us (0.72)
  the two profiles are of different devices: /device:TPU:4 before, /device:TPU:1 now
where the time goes in v2:
time: 50.9 us; the launch traced here: 50.6 us
  Pallas kernels  49.6 us (97%)
  local copies, waits for them, and re-layouts  0.97 us (2%)
    pallas_call x1, Pallas kernels, body(): pl.pallas_call(functools.partial(kernel, pi_count, pj_count), in_specs=[h...  49.6 us

profile of v2, /device:TPU:1, one launch (start us, length us, event | category | flops | bytes accessed | tf_op | source)
XLA Modules:
  0.0 50.6 jit_solution(3668269128913825945)
XLA Ops:
  0.0 49.6 %layer.1 = bf16[32,64,256]{2,1,0:T(8,128)(2,1)S(1)} custom-call(bf16[256,128,128]{2,1,0:T(8,128)(2,1)} %pair_hbm.1, f32[8,128]{1,0:T(8,128)} %bitcast.5, bf16[32,64,256]{2,1,0:T(8,128)(2,1)} %msa_hbm.1, f32[1,64]{1,0:T(1,128)} %bitcast.6, f32[1,64]{1,0:T(1,128)} %bitcast.7, bf16[64,256]{1,0:T(8,128)(2,1)} %payload_ref.1, bf16[64,256]{1,0:T(8,128)(2,1)} %switch_ref.1, ...), custom_call_target="tpu_custom_call" | custom-call | tf_op jit(solution)/shard_map/layer/pallas_call | solution.py:428
  49.6 1.0 %copy.10 = bf16[32,64,256]{2,1,0:T(8,128)(2,1)} copy(bf16[32,64,256]{2,1,0:T(8,128)(2,1)S(1)} %layer.1) | data formatting | bytes 2097152

commit v3 on v2

--- a/solution.py
+++ b/solution.py
@@ -14,8 +14,10 @@
 TILE = 16
 CHUNK = 32
 GROUP = 16
+AHEAD = 3
+SLOTS = 4
 HELD = 3
-VMEM_LIMIT = 58 << 20
+VMEM_LIMIT = 61 << 20
 
 
 def dot(a, b, dims=(((1,), (0,)), ((), ()))):
@@ -30,17 +32,31 @@
     return w3.astype(jnp.bfloat16)
 
 
-def tile_scores(x, w3):
+def tile_scores(x, w3, centring):
     rows, cols, chans = x.shape
     heads = w3.shape[0] // 4
     x = x.reshape(rows * cols, chans)
-    mean = dot(x, jnp.ones((chans, chans), jnp.bfloat16)) * (1.0 / chans)
-    centred = x.astype(jnp.float32) - mean
+    half = rows * cols // 2
+    centred = dot(jnp.concatenate([x[:half], x[half:]], axis=1), centring)
     square = centred * centred
-    top = square.astype(jnp.bfloat16)
-    rest = (square - top.astype(jnp.float32)).astype(jnp.bfloat16)
-    ones = jnp.ones((2 * heads, 2 * chans), jnp.bfloat16)
-    variance = dot(ones, jnp.concatenate([top, rest], axis=1), NT)[:heads] * (1.0 / chans)
+    one, two = square[:, :chans], square[:, chans:]
+    lane = lax.broadcasted_iota(jnp.int32, one.shape, 1)
+    low = lane < chans // 2
+    both = jnp.where(low, one, two) + pltpu.roll(jnp.where(low, two, one), chans // 2, 1)
+    one, two = both[: half // 2], both[half // 2 :]
+    quarter = chans // 4
+    low = lane[: half // 2] % (2 * quarter) < quarter
+    both = jnp.where(
+        low, one + pltpu.roll(one, chans - quarter, 1), two + pltpu.roll(two, quarter, 1)
+    )
+    top = both.astype(jnp.bfloat16)
+    rest = (both - top.astype(jnp.float32)).astype(jnp.bfloat16)
+    group = lax.broadcasted_iota(jnp.int32, (4 * heads, 2 * chans), 0) // heads
+    owner = lax.broadcasted_iota(jnp.int32, (4 * heads, 2 * chans), 1) % chans // quarter
+    picks = jnp.where(group == owner, 1.0, 0.0).astype(jnp.bfloat16)
+    sums = dot(picks, jnp.concatenate([top, rest], axis=1), NT)
+    sums = [sums[g * heads : (g + 1) * heads] for g in range(4)]
+    variance = jnp.concatenate(sums, axis=1) * (1.0 / chans)
     parts = dot(w3, x, NT)
     scores = parts[:heads] + (parts[heads : 2 * heads] + parts[2 * heads : 3 * heads])
     return scores * lax.rsqrt(variance + EPS)
@@ -61,12 +77,13 @@
     wv_ref,
     ws_ref,
     spread,
+    centring,
     pair,
     msa,
     ex,
     hold,
     peaks,
-    scale,
+    turned,
     vals,
     weights,
     acc,
@@ -84,6 +101,7 @@
     ms_sx,
     ms_up,
     ms_dn,
+    rounds,
 ):
     me_i, me_j = lax.axis_index("pi"), lax.axis_index("pj")
     line, yline = pj_count // CORES, pi_count // 2
@@ -99,7 +117,7 @@
     x_near = me_i - x + (1 - x)
 
     pair_in = lambda q: pltpu.make_async_copy(
-        pair_hbm.at[pl.ds(q * CHUNK, CHUNK)], pair.at[q], pair_sem.at[q]
+        pair_hbm.at[pl.ds(q * CHUNK, CHUNK)], pair.at[q % AHEAD], pair_sem.at[q % AHEAD]
     )
     own_in = [
         pltpu.make_async_copy(msa_hbm.at[pl.ds(h * half, half)], msa.at[me_i * 2 + h], msa_sem.at[h])
@@ -107,20 +125,29 @@
     ]
     for h in range(2):
         own_in[h].start()
-    lax.fori_loop(0, chunks, lambda q, c: (pair_in(q).start(), c)[1], 0)
+    lax.fori_loop(0, AHEAD, lambda q, c: (pair_in(q).start(), c)[1], 0)
 
     barrier = pltpu.get_barrier_semaphore()
 
     def greet(i, j):
         pl.semaphore_signal(barrier, inc=1, device_id=(i, j), device_id_type=MESH)
 
-    lax.fori_loop(1, pj_count, lambda r, c: (greet(me_i, (me_j + r) % pj_count), c)[1], 0)
+    up_y, down_y = y < yline - 1, y > 0
+    up_z, down_z = z < line - 1, z > 0
+    near_z = 1 + jnp.where(up_z, 1, 0) + jnp.where(down_z, 1, 0)
+    near_y = jnp.where(up_y, 1, 0) + jnp.where(down_y, 1, 0)
+
+    def tell_line(tell):
+        tell(me_i, mate)
+        pl.when(up_z)(lambda: tell(me_i, me_j + CORES))
+        pl.when(down_z)(lambda: tell(me_i, me_j - CORES))
+
+    tell_line(greet)
     greet(x_near, me_j)
-    up_y, down_y = y < yline - 1, y > 0
     pl.when(up_y)(lambda: greet(me_i + 2, me_j))
     pl.when(down_y)(lambda: greet(me_i - 2, me_j))
 
-    pl.semaphore_wait(barrier, pj_count + jnp.where(up_y, 1, 0) + jnp.where(down_y, 1, 0))
+    pl.semaphore_wait(barrier, 1 + near_y + near_z)
 
     def msa_copy(p, h, send, i, count=1):
         part = msa.at[pl.ds(p * 2 + h, count)]
@@ -194,9 +221,15 @@
         return ex_along(me_j, q, ex_dn, me_j - CORES)
 
     def ex_mate(o, q=None):
-        return ex_copy(o, q, ex_pt.at[o // CORES], ex_far.at[o // CORES], mate)
-
-    up_z, down_z = z < line - 1, z > 0
+        late = 0 if q is None else jnp.where(q >= chunks - HELD, 1, 0)
+        return ex_copy(o, q, ex_pt.at[o // CORES], ex_far.at[o // CORES, late], mate)
+
+    def ex_mate_part(o, late):
+        block = ex.at[o, pl.ds(chunks - HELD, HELD) if late else pl.ds(0, chunks - HELD)]
+        c = o // CORES
+        return pltpu.make_async_remote_copy(
+            block, block, ex_pt.at[c], ex_far.at[c, late], device_id=(me_i, mate), device_id_type=MESH
+        )
 
     def send_own(q):
         pl.when(up_z)(lambda: ex_up(me_j, q).start())
@@ -233,7 +266,22 @@
     def others(f):
         lax.fori_loop(1, pj_count, lambda r, c: (f((me_j + r) % pj_count), c)[1], 0)
 
+    def tell_round(r):
+        def tell(i, j):
+            pl.semaphore_signal(rounds.at[r], inc=1, device_id=(i, j), device_id_type=MESH)
+
+        tell_line(tell)
+
+    def hear_round(r):
+        pl.semaphore_wait(rounds.at[r], near_z)
+
+    tell_round(0)
     w3 = split_weights(w_ref[...])
+    pair_chans = w3.shape[1]
+    across = lax.broadcasted_iota(jnp.int32, centring.shape, 0)
+    along = lax.broadcasted_iota(jnp.int32, centring.shape, 1)
+    away = jnp.where(across // pair_chans == along // pair_chans, -1.0 / pair_chans, 0.0)
+    centring[...] = jnp.where(across == along, 1.0 + away, away).astype(jnp.bfloat16)
     lane = lax.broadcasted_iota(jnp.int32, (heads, rows), 1)
     peaks[me_j] = jnp.zeros((heads, rows), jnp.float32)
 
@@ -241,7 +289,7 @@
         pair_in(q).wait()
         top = peaks[me_j]
         for t in range(CHUNK // TILE):
-            scores = tile_scores(pair[q, t * TILE : (t + 1) * TILE], w3)
+            scores = tile_scores(pair[q % AHEAD, t * TILE : (t + 1) * TILE], w3, centring[...])
             for k in range(TILE):
                 one = scores[:, k * cols : (k + 1) * cols]
                 peak = jnp.max(one, axis=1, keepdims=True)
@@ -249,8 +297,20 @@
                 top = jnp.where(lane == q * CHUNK + t * TILE + k, peak, top)
         peaks[me_j] = top
         ex[me_j, q] = hold[...].astype(jnp.bfloat16)
-
-    lax.fori_loop(0, chunks, lambda q, c: (pair_chunk(q), send_own(q), c)[2], 0)
+        pl.when(q + AHEAD < chunks)(lambda: pair_in(q + AHEAD).start())
+
+    def pair_step(q, carry):
+        pair_chunk(q)
+        send_own(q)
+
+        @pl.when(q < line - 1)
+        def _():
+            hear_round(q)
+            pl.when(q < line - 2)(lambda: tell_round(q + 1))
+
+        return carry
+
+    lax.fori_loop(0, chunks, pair_step, 0)
     others(lambda j: peak_copy(me_j, j).start())
 
     def relays(d, first, last):
@@ -281,7 +341,7 @@
     relays(1, chunks - 2, chunks)
     first_relays()
 
-    for slot in range(2):
+    for slot in range(SLOTS):
         vals[slot, :, span:, :] = jnp.ones((heads, 16, rows), jnp.bfloat16)
 
     def zero_head(h, carry):
@@ -290,33 +350,52 @@
 
     lax.fori_loop(0, heads, zero_head, 0)
 
-    all_peaks().wait_recv()
-    scale[...] = jnp.exp(peaks[...] - jnp.max(peaks[...], axis=0, keepdims=True))
-
-    def values(p, slot):
-        pl.when(p % 2 != x)(lambda: take(p, 1))
-
+    def values(p, h, slot):
         def value_group(g, carry):
             for k in range(GROUP):
                 s = g * GROUP + k
                 v = dot(wv_ref[...], normed(p, s)).astype(jnp.bfloat16)
                 at = pl.ds(pl.multiple_of(s * width, width), width)
-                for h in range(heads):
-                    vals[slot, h, at, :] = v[h * width : (h + 1) * width]
+                for n in range(heads):
+                    vals[slot, n, at, :] = v[n * width : (n + 1) * width]
             return carry
 
-        lax.fori_loop(0, seqs // GROUP, value_group, 0)
-
-    def rescale(p, slot):
-        ex_mate(p * CORES + (1 - core)).wait_recv()
-        both = scale[pl.ds(p * CORES, CORES)].reshape(CORES * heads, rows)
-        pad = jnp.zeros((128 - CORES * heads, rows), jnp.float32)
-        turned = jnp.concatenate([both, pad], axis=0).T
-        for h in range(heads):
-            for c in range(CORES):
-                e = ex[p * CORES + c, :, h].reshape(rows, cols).astype(jnp.float32)
-                e = e * turned[:, c * heads + h : c * heads + h + 1]
-                weights[slot, h, :, c * cols : (c + 1) * cols] = e.astype(jnp.bfloat16)
+        steps = half // GROUP
+        lax.fori_loop(h * steps, (h + 1) * steps, value_group, 0)
+
+    y_near = (y + 1) % yline * 2 + x
+
+    def slot_of(p):
+        return jnp.where(p == me_i, 0, jnp.where(p == x_near, 1, jnp.where(p == y_near, 2, 3)))
+
+    def early_values(k, carry):
+        p = jnp.where(k < 2, me_i, jnp.where(k == 2, x_near, y_near))
+        h = jnp.where((k == 1) | (k == 3), 1, 0)
+        values(p, h, slot_of(p))
+        return carry
+
+    lax.fori_loop(0, 4, early_values, 0)
+
+    all_peaks().wait_recv()
+    top = jnp.max(peaks[...], axis=0)
+
+    def turn(o, carry):
+        pad = jnp.zeros((128 - heads, rows), jnp.float32)
+        turned[o] = jnp.concatenate([jnp.exp(peaks[o] - top), pad], axis=0).T
+        return carry
+
+    lax.fori_loop(0, pj_count, turn, 0)
+
+    def rescale(p, slot, late):
+        first, last = (chunks - HELD, chunks) if late else (0, chunks - HELD)
+        ex_mate_part(p * CORES + (1 - core), late).wait_recv()
+        span_rows = slice(first * CHUNK, last * CHUNK)
+        for c in range(CORES):
+            o = p * CORES + c
+            for h in range(heads):
+                e = ex[o, first:last, h].reshape((last - first) * CHUNK, cols).astype(jnp.float32)
+                e = (e * turned[o, span_rows, h : h + 1]).astype(jnp.bfloat16)
+                weights[slot, h, span_rows, c * cols : (c + 1) * cols] = e
 
     def attend(slot, weight_slot):
         for h in range(heads):
@@ -334,8 +413,9 @@
         return jnp.where(apart(p) == line - 1, line, unit)
 
     def value_unit(p):
-        early = jnp.where(crosses(p), line - 1, line - 2)
-        return jnp.where(apart(p) == line - 1, early, attend_unit(p))
+        late = line - 1 if pi_count <= SLOTS else attend_unit(p)
+        late = jnp.where(crosses(p), late, attend_unit(p))
+        return jnp.where(p == me_i, -1, jnp.where((p == x_near) | (p == y_near), 1, late))
 
     half_way = chunks // 2
     diagonal_block = (y + 1) % yline * 2 + (1 - x)
@@ -361,20 +441,33 @@
         @pl.when(fresh & (u == line - 1))
         def _():
             relays(line - 1, 0, chunks - HELD)
+            farthest = jnp.where(z == 0, line - 1, 0)
+            pl.when((z == 0) | (z == line - 1))(lambda: rescale(farthest, 1, 0))
             for e in range(1, yline):
                 pass_y(e, 1 - x, 0, False)
 
-        @pl.when(fresh & (u == line))
+        last = apart(p) == line - 1
+        early = (p == diagonal_block) & jnp.logical_not(last)
+        weight_slot = jnp.where(early, 2, jnp.where(last, 1, 0))
+        rescale_unit = jnp.where(early, line - 2, attend_unit(p))
+
+        @pl.when(value_unit(p) == u)
+        def _():
+            pl.when(p % 2 != x)(lambda: take(p, 1))
+            first = jnp.where(p == x_near, 1, 0)
+            end = jnp.where(p == y_near, 1, 2)
+            lax.fori_loop(first, end, lambda h, c: (values(p, h, slot_of(p)), c)[1], 0)
+
+        @pl.when((u == line - 1) & (p == diagonal_block))
         def _():
             relays(line - 1, chunks - HELD, chunks)
 
-        slot = jnp.where(apart(p) == line - 1, 1, 0)
-        early = (p == diagonal_block) & (slot == 0)
-        weight_slot = jnp.where(early, 2, slot)
-        rescale_unit = jnp.where(early, line - 2, attend_unit(p))
-        pl.when(value_unit(p) == u)(lambda: values(p, slot))
-        pl.when(rescale_unit == u)(lambda: rescale(p, weight_slot))
-        pl.when(attend_unit(p) == u)(lambda: attend(slot, weight_slot))
+        @pl.when(rescale_unit == u)
+        def _():
+            pl.when(jnp.logical_not(last))(lambda: rescale(p, weight_slot, 0))
+            rescale(p, weight_slot, 1)
+
+        pl.when(attend_unit(p) == u)(lambda: attend(slot_of(p), weight_slot))
         return carry
 
     lax.fori_loop(0, (line + 1) * pi_count, step, 0)
@@ -434,29 +527,31 @@
             pltpu.VMEM((joint, chans), jnp.bfloat16),
             pltpu.VMEM((joint, chans), jnp.bfloat16),
             pltpu.VMEM((2, chans, rows), jnp.float32),
-            pltpu.VMEM((chunks, CHUNK, cols, pair_chans), jnp.bfloat16),
+            pltpu.VMEM((2 * pair_chans, 2 * pair_chans), jnp.bfloat16),
+            pltpu.VMEM((AHEAD, CHUNK, cols, pair_chans), jnp.bfloat16),
             pltpu.VMEM((pi_count * 2, seqs // 2, chans, tokens), jnp.bfloat16),
             pltpu.VMEM((pj_count, chunks, heads, CHUNK, cols), jnp.bfloat16),
             pltpu.VMEM((heads, CHUNK, cols), jnp.float32),
             pltpu.VMEM((pj_count, heads, rows), jnp.float32),
-            pltpu.VMEM((pj_count, heads, rows), jnp.float32),
-            pltpu.VMEM((2, heads, span + 16, rows), jnp.bfloat16),
+            pltpu.VMEM((pj_count, rows, 128), jnp.float32),
+            pltpu.VMEM((SLOTS, heads, span + 16, rows), jnp.bfloat16),
             pltpu.VMEM((3, heads, rows, CORES * cols), jnp.bfloat16),
             pltpu.VMEM((heads, span + 16, rows), jnp.float32),
             pltpu.VMEM((seqs, joint, tokens), jnp.float32),
-            dma((chunks,)),
+            dma((AHEAD,)),
             dma((2,)),
             dma((pj_count // CORES, chunks)),
             dma((pj_count // CORES,)),
             dma,
             dma((pj_count // CORES,)),
-            dma((pj_count // CORES,)),
+            dma((pj_count // CORES, 2)),
             dma,
             dma,
             dma((pi_count, 2)),
             dma,
             dma((pi_count // 2,)),
             dma((pi_count // 2,)),
+            pltpu.SemaphoreType.REGULAR((pj_count // CORES - 1,)),
         ],
         compiler_params=pltpu.CompilerParams(
             collective_id=0, has_side_effects=True, vmem_limit_bytes=VMEM_LIMIT

time: 50.9 us -> 48.6 us (0.955)
  Pallas kernels: 49.6 us -> 47.2 us
    pallas_call x1, Pallas kernels: 49.6 us -> 47.2 us  [body(): pl.pallas_call(functools.partial(kernel, pi_count, pj_count), in_specs=[h...]
where the time goes in v3:
time: 48.6 us; the launch traced here: 48.2 us
  Pallas kernels  47.2 us (97%)
  local copies, waits for them, and re-layouts  0.97 us (2%)
    pallas_call x1, Pallas kernels, body(): pl.pallas_call(functools.partial(kernel, pi_count, pj_count), in_specs=[h...  47.2 us
    unnamed x1, local copies, waits for them, and re-layouts  0.97 us

profile of v3, /device:TPU:1, one launch (start us, length us, event | category | flops | bytes accessed | tf_op | source)
XLA Modules:
  0.0 48.2 jit_solution(9330286982228323125)
XLA Ops:
  0.0 47.2 %layer.1 = bf16[32,64,256]{2,1,0:T(8,128)(2,1)S(1)} custom-call(bf16[256,128,128]{2,1,0:T(8,128)(2,1)} %pair_hbm.1, f32[8,128]{1,0:T(8,128)} %bitcast.5, bf16[32,64,256]{2,1,0:T(8,128)(2,1)} %msa_hbm.1, f32[1,64]{1,0:T(1,128)} %bitcast.6, f32[1,64]{1,0:T(1,128)} %bitcast.7, bf16[64,256]{1,0:T(8,128)(2,1)} %payload_ref.1, bf16[64,256]{1,0:T(8,128)(2,1)} %switch_ref.1, ...), custom_call_target="tpu_custom_call" | custom-call | tf_op jit(solution)/shard_map/layer/pallas_call | solution.py:521
  47.2 1.0 %copy.10 = bf16[32,64,256]{2,1,0:T(8,128)(2,1)} copy(bf16[32,64,256]{2,1,0:T(8,128)(2,1)S(1)} %layer.1) | data formatting | bytes 2097152

commit v4 on v3

--- a/solution.py
+++ b/solution.py
@@ -12,10 +12,12 @@
 NT = (((1,), (1,)), ((), ()))
 CORES = 2
 TILE = 16
+PIECE = 32
 CHUNK = 32
 GROUP = 16
 AHEAD = 3
 SLOTS = 4
+SOON = 5
 HELD = 3
 VMEM_LIMIT = 61 << 20
 
@@ -66,14 +68,20 @@
     pi_count,
     pj_count,
     pair_hbm,
+    w_hbm,
+    msa_hbm,
+    gain_hbm,
+    shift_hbm,
+    payload_hbm,
+    switch_hbm,
+    wc_hbm,
+    out_ref,
     w_ref,
-    msa_hbm,
     gain_ref,
     shift_ref,
     payload_ref,
     switch_ref,
     wc_ref,
-    out_ref,
     wv_ref,
     ws_ref,
     spread,
@@ -88,6 +96,8 @@
     weights,
     acc,
     gate,
+    w_sem,
+    small_sem,
     pair_sem,
     msa_sem,
     ex_rs,
@@ -110,6 +120,7 @@
     chunks = ex.shape[1]
     heads, cols = ex.shape[2], ex.shape[4]
     rows = chunks * CHUNK
+    share = CHUNK // PIECE
     seqs, half, chans = out_ref.shape[0], msa.shape[1], msa.shape[2]
     span = vals.shape[2] - 16
     width = span // seqs
@@ -117,15 +128,31 @@
     x_near = me_i - x + (1 - x)
 
     pair_in = lambda q: pltpu.make_async_copy(
-        pair_hbm.at[pl.ds(q * CHUNK, CHUNK)], pair.at[q % AHEAD], pair_sem.at[q % AHEAD]
+        pair_hbm.at[pl.ds(q * PIECE, PIECE)], pair.at[q % AHEAD], pair_sem.at[q % AHEAD]
     )
     own_in = [
         pltpu.make_async_copy(msa_hbm.at[pl.ds(h * half, half)], msa.at[me_i * 2 + h], msa_sem.at[h])
         for h in range(2)
     ]
+    w_in = pltpu.make_async_copy(w_hbm, w_ref, w_sem)
+    w_in.start()
     for h in range(2):
         own_in[h].start()
     lax.fori_loop(0, AHEAD, lambda q, c: (pair_in(q).start(), c)[1], 0)
+    small_in = [
+        pltpu.make_async_copy(source, target, small_sem.at[k])
+        for k, (source, target) in enumerate(
+            (
+                (gain_hbm, gain_ref),
+                (shift_hbm, shift_ref),
+                (payload_hbm, payload_ref),
+                (switch_hbm, switch_ref),
+                (wc_hbm, wc_ref),
+            )
+        )
+    ]
+    for copy in small_in:
+        copy.start()
 
     barrier = pltpu.get_barrier_semaphore()
 
@@ -276,6 +303,7 @@
         pl.semaphore_wait(rounds.at[r], near_z)
 
     tell_round(0)
+    w_in.wait()
     w3 = split_weights(w_ref[...])
     pair_chans = w3.shape[1]
     across = lax.broadcasted_iota(jnp.int32, centring.shape, 0)
@@ -285,32 +313,41 @@
     lane = lax.broadcasted_iota(jnp.int32, (heads, rows), 1)
     peaks[me_j] = jnp.zeros((heads, rows), jnp.float32)
 
-    def pair_chunk(q):
+    def pair_piece(q):
         pair_in(q).wait()
         top = peaks[me_j]
-        for t in range(CHUNK // TILE):
+        for t in range(PIECE // TILE):
             scores = tile_scores(pair[q % AHEAD, t * TILE : (t + 1) * TILE], w3, centring[...])
             for k in range(TILE):
                 one = scores[:, k * cols : (k + 1) * cols]
                 peak = jnp.max(one, axis=1, keepdims=True)
                 hold[:, t * TILE + k, :] = jnp.exp(one - peak)
-                top = jnp.where(lane == q * CHUNK + t * TILE + k, peak, top)
+                top = jnp.where(lane == q * PIECE + t * TILE + k, peak, top)
         peaks[me_j] = top
-        ex[me_j, q] = hold[...].astype(jnp.bfloat16)
-        pl.when(q + AHEAD < chunks)(lambda: pair_in(q + AHEAD).start())
+        at = pl.ds(pl.multiple_of(q % share * PIECE, PIECE), PIECE)
+        ex[me_j, q // share, :, at, :] = hold[...].astype(jnp.bfloat16)
+        pl.when(q + AHEAD < chunks * share)(lambda: pair_in(q + AHEAD).start())
+
+    soon = min(line - 1, (chunks * share - 2) // 2)
+
+    def next_round(r):
+        hear_round(r)
+        pl.when(r < line - 2)(lambda: tell_round(r + 1))
 
     def pair_step(q, carry):
-        pair_chunk(q)
-        send_own(q)
-
-        @pl.when(q < line - 1)
-        def _():
-            hear_round(q)
-            pl.when(q < line - 2)(lambda: tell_round(q + 1))
-
-        return carry
-
-    lax.fori_loop(0, chunks, pair_step, 0)
+        pair_piece(q)
+        pl.when(q % share == share - 1)(lambda: send_own(q // share))
+
+        pl.when((q >= SOON) & (q % 2 == 1))(lambda: relay(1, (q - SOON) // 2))
+
+        @pl.when((q % 2 == 1) & (q >= 3) & (q < 3 + 2 * soon))
+        def _():
+            next_round((q - 3) // 2)
+
+        return carry
+
+    lax.fori_loop(0, chunks * share, pair_step, 0)
+    lax.fori_loop(soon, line - 1, lambda r, c: (next_round(r), c)[1], 0)
     others(lambda j: peak_copy(me_j, j).start())
 
     def relays(d, first, last):
@@ -328,6 +365,8 @@
             gate[s] = jax.nn.sigmoid(dot(ws_ref[...], normed(me_i, s)))
         return carry
 
+    for copy in small_in:
+        copy.wait()
     wv_ref[...] = payload_ref[...].astype(jnp.float32).T.astype(jnp.bfloat16)
     ws_ref[...] = switch_ref[...].astype(jnp.float32).T.astype(jnp.bfloat16)
     diagonal = lax.broadcasted_iota(jnp.int32, (chans, chans), 0)
@@ -336,7 +375,7 @@
         column = jnp.sum(jnp.where(diagonal, ref[...], 0.0), axis=1, keepdims=True)
         spread[k] = jnp.broadcast_to(column, (chans, rows))
 
-    relays(1, 0, chunks - 2)
+    relays(1, (chunks - SOON + 1) // 2, chunks - 2)
     lax.fori_loop(0, seqs // GROUP, gate_group, 0)
     relays(1, chunks - 2, chunks)
     first_relays()
@@ -407,15 +446,22 @@
     def crosses(p):
         return (p // 2 != y) & (p % 2 != x)
 
+    def farthest_from_here(p):
+        return apart(p) == line - 1
+
     def attend_unit(p):
         near = jnp.where(apart(p) <= 1, jnp.where(p == me_i, 0, 1), apart(p))
-        unit = jnp.where(crosses(p), line - 1, near)
-        return jnp.where(apart(p) == line - 1, line, unit)
+        return jnp.where(crosses(p) | farthest_from_here(p), -1, near)
 
     def value_unit(p):
-        late = line - 1 if pi_count <= SLOTS else attend_unit(p)
-        late = jnp.where(crosses(p), late, attend_unit(p))
-        return jnp.where(p == me_i, -1, jnp.where((p == x_near) | (p == y_near), 1, late))
+        beside = (p == x_near) | (p == y_near)
+        return jnp.where(p == me_i, -1, jnp.where(beside, 1, attend_unit(p)))
+
+    def late_values(p):
+        pl.when(p % 2 != x)(lambda: take(p, 1))
+        first = jnp.where(p == x_near, 1, 0)
+        end = jnp.where(p == y_near, 1, 2)
+        lax.fori_loop(first, end, lambda h, c: (values(p, h, slot_of(p)), c)[1], 0)
 
     half_way = chunks // 2
     diagonal_block = (y + 1) % yline * 2 + (1 - x)
@@ -434,43 +480,58 @@
         def _():
             relay(2, half_way + p)
 
-        @pl.when(fresh & (u >= 3) & (u < line - 1))
+        @pl.when(fresh & (u >= 3))
         def _():
             relays(u, 0, chunks)
 
-        @pl.when(fresh & (u == line - 1))
-        def _():
-            relays(line - 1, 0, chunks - HELD)
-            farthest = jnp.where(z == 0, line - 1, 0)
-            pl.when((z == 0) | (z == line - 1))(lambda: rescale(farthest, 1, 0))
-            for e in range(1, yline):
-                pass_y(e, 1 - x, 0, False)
-
-        last = apart(p) == line - 1
-        early = (p == diagonal_block) & jnp.logical_not(last)
-        weight_slot = jnp.where(early, 2, jnp.where(last, 1, 0))
-        rescale_unit = jnp.where(early, line - 2, attend_unit(p))
-
-        @pl.when(value_unit(p) == u)
-        def _():
-            pl.when(p % 2 != x)(lambda: take(p, 1))
-            first = jnp.where(p == x_near, 1, 0)
-            end = jnp.where(p == y_near, 1, 2)
-            lax.fori_loop(first, end, lambda h, c: (values(p, h, slot_of(p)), c)[1], 0)
-
-        @pl.when((u == line - 1) & (p == diagonal_block))
-        def _():
-            relays(line - 1, chunks - HELD, chunks)
-
-        @pl.when(rescale_unit == u)
-        def _():
-            pl.when(jnp.logical_not(last))(lambda: rescale(p, weight_slot, 0))
-            rescale(p, weight_slot, 1)
-
-        pl.when(attend_unit(p) == u)(lambda: attend(slot_of(p), weight_slot))
-        return carry
-
-    lax.fori_loop(0, (line + 1) * pi_count, step, 0)
+        pl.when(value_unit(p) == u)(lambda: late_values(p))
+
+        @pl.when(attend_unit(p) == u)
+        def _():
+            rescale(p, 0, 0)
+            rescale(p, 0, 1)
+            attend(slot_of(p), 0)
+
+        return carry
+
+    lax.fori_loop(0, (line - 1) * pi_count, step, 0)
+
+    at_end = (z == 0) | (z == line - 1)
+    farthest = jnp.where(z == 0, line - 1, 0)
+
+    @pl.when(jnp.logical_not(farthest_from_here(diagonal_block)))
+    def _():
+        rescale(diagonal_block, 2, 0)
+        rescale(diagonal_block, 2, 1)
+
+    relays(line - 1, 0, chunks - HELD)
+    for e in range(1, yline):
+        pass_y(e, 1 - x, 0, False)
+    for e in range(1, yline):
+        p = (y + e) % yline * 2 + (1 - x)
+        here = jnp.logical_not(farthest_from_here(p))
+        if pi_count <= SLOTS:
+            late_values(p)
+        else:
+            pl.when(here)(lambda: late_values(p))
+        if e == 1:
+            relays(line - 1, chunks - HELD, chunks - 1)
+            pl.when(at_end)(lambda: rescale(farthest, 1, 0))
+            relay(line - 1, chunks - 1)
+
+        @pl.when(here)
+        def _():
+            if e > 1:
+                rescale(p, 0, 0)
+                rescale(p, 0, 1)
+            attend(slot_of(p), 2 if e == 1 else 0)
+
+    @pl.when(at_end)
+    def _():
+        if pi_count > SLOTS:
+            pl.when(slot_of(farthest) == 3)(lambda: late_values(farthest))
+        rescale(farthest, 1, 1)
+        attend(slot_of(farthest), 1)
 
     inverse = 1.0 / acc[:, span : span + 8, :]
     inverse = inverse[:, :1, :]
@@ -479,8 +540,8 @@
         for k in range(GROUP):
             s = g * GROUP + k
             at = pl.ds(pl.multiple_of(s * width, width), width)
-            share = gate[s].reshape(heads, width, rows)
-            mixed = (share * (acc[:, at, :] * inverse)).astype(jnp.bfloat16)
+            opened = gate[s].reshape(heads, width, rows)
+            mixed = (opened * (acc[:, at, :] * inverse)).astype(jnp.bfloat16)
             out_ref[s] = dot(wc_ref[...], mixed.reshape(heads * width, rows)).astype(jnp.bfloat16)
         return carry
 
@@ -520,24 +581,32 @@
     dma = pltpu.SemaphoreType.DMA
     return pl.pallas_call(
         functools.partial(kernel, pi_count, pj_count),
-        in_specs=[hbm, vmem, hbm] + [vmem] * 5,
+        in_specs=[hbm] * 8,
         out_specs=vmem,
         out_shape=pltpu.VMEM(aligned.shape, jnp.bfloat16),
         scratch_shapes=[
+            pltpu.VMEM((heads, pair_chans), jnp.float32),
+            pltpu.VMEM((1, chans), jnp.float32),
+            pltpu.VMEM((1, chans), jnp.float32),
+            pltpu.VMEM(payload_w.shape, jnp.bfloat16),
+            pltpu.VMEM(switch_w.shape, jnp.bfloat16),
+            pltpu.VMEM(closing_w.shape[::-1], jnp.bfloat16),
             pltpu.VMEM((joint, chans), jnp.bfloat16),
             pltpu.VMEM((joint, chans), jnp.bfloat16),
             pltpu.VMEM((2, chans, rows), jnp.float32),
             pltpu.VMEM((2 * pair_chans, 2 * pair_chans), jnp.bfloat16),
-            pltpu.VMEM((AHEAD, CHUNK, cols, pair_chans), jnp.bfloat16),
+            pltpu.VMEM((AHEAD, PIECE, cols, pair_chans), jnp.bfloat16),
             pltpu.VMEM((pi_count * 2, seqs // 2, chans, tokens), jnp.bfloat16),
             pltpu.VMEM((pj_count, chunks, heads, CHUNK, cols), jnp.bfloat16),
-            pltpu.VMEM((heads, CHUNK, cols), jnp.float32),
+            pltpu.VMEM((heads, PIECE, cols), jnp.float32),
             pltpu.VMEM((pj_count, heads, rows), jnp.float32),
             pltpu.VMEM((pj_count, rows, 128), jnp.float32),
             pltpu.VMEM((SLOTS, heads, span + 16, rows), jnp.bfloat16),
             pltpu.VMEM((3, heads, rows, CORES * cols), jnp.bfloat16),
             pltpu.VMEM((heads, span + 16, rows), jnp.float32),
             pltpu.VMEM((seqs, joint, tokens), jnp.float32),
+            dma,
+            dma((5,)),
             dma((AHEAD,)),
             dma((2,)),
             dma((pj_count // CORES, chunks)),

time: 48.6 us -> 47.4 us (0.975)
  Pallas kernels: 47.2 us -> 46.3 us
    pallas_call x1, Pallas kernels: 47.2 us -> 46.3 us  [body(): pl.pallas_call(functools.partial(kernel, pi_count, pj_count), in_specs=[h...]
where the time goes in v4:
time: 47.4 us; the launch traced here: 47.3 us
  Pallas kernels  46.3 us (98%)
  local copies, waits for them, and re-layouts  0.97 us (2%)
    pallas_call x1, Pallas kernels, body(): pl.pallas_call(functools.partial(kernel, pi_count, pj_count), in_specs=[h...  46.3 us
    unnamed x1, local copies, waits for them, and re-layouts  0.97 us

profile of v4, /device:TPU:1, one launch (start us, length us, event | category | flops | bytes accessed | tf_op | source)
XLA Modules:
  0.0 47.3 jit_solution(15561021951502766591)
XLA Ops:
  0.0 46.3 %layer.1 = bf16[32,64,256]{2,1,0:T(8,128)(2,1)S(1)} custom-call(bf16[256,128,128]{2,1,0:T(8,128)(2,1)} %pair_hbm.1, f32[8,128]{1,0:T(8,128)} %bitcast.5, bf16[32,64,256]{2,1,0:T(8,128)(2,1)} %msa_hbm.1, f32[1,64]{1,0:T(1,128)} %bitcast.6, f32[1,64]{1,0:T(1,128)} %bitcast.7, bf16[64,256]{1,0:T(8,128)(2,1)} %payload_hbm.1, bf16[64,256]{1,0:T(8,128)(2,1)} %switch_hbm.1, ...), custom_call_target="tpu_custom_call" | custom-call | tf_op jit(solution)/shard_map/layer/pallas_call | solution.py:582
  46.3 1.0 %copy.10 = bf16[32,64,256]{2,1,0:T(8,128)(2,1)} copy(bf16[32,64,256]{2,1,0:T(8,128)(2,1)S(1)} %layer.1) | data formatting | bytes 2097152

commit v5 on v4

--- a/solution.py
+++ b/solution.py
@@ -42,22 +42,15 @@
     centred = dot(jnp.concatenate([x[:half], x[half:]], axis=1), centring)
     square = centred * centred
     one, two = square[:, :chans], square[:, chans:]
-    lane = lax.broadcasted_iota(jnp.int32, one.shape, 1)
-    low = lane < chans // 2
+    low = lax.broadcasted_iota(jnp.int32, one.shape, 1) < chans // 2
     both = jnp.where(low, one, two) + pltpu.roll(jnp.where(low, two, one), chans // 2, 1)
-    one, two = both[: half // 2], both[half // 2 :]
-    quarter = chans // 4
-    low = lane[: half // 2] % (2 * quarter) < quarter
-    both = jnp.where(
-        low, one + pltpu.roll(one, chans - quarter, 1), two + pltpu.roll(two, quarter, 1)
-    )
     top = both.astype(jnp.bfloat16)
     rest = (both - top.astype(jnp.float32)).astype(jnp.bfloat16)
-    group = lax.broadcasted_iota(jnp.int32, (4 * heads, 2 * chans), 0) // heads
-    owner = lax.broadcasted_iota(jnp.int32, (4 * heads, 2 * chans), 1) % chans // quarter
+    group = lax.broadcasted_iota(jnp.int32, (2 * heads, 2 * chans), 0) // heads
+    owner = lax.broadcasted_iota(jnp.int32, (2 * heads, 2 * chans), 1) % chans // (chans // 2)
     picks = jnp.where(group == owner, 1.0, 0.0).astype(jnp.bfloat16)
     sums = dot(picks, jnp.concatenate([top, rest], axis=1), NT)
-    sums = [sums[g * heads : (g + 1) * heads] for g in range(4)]
+    sums = [sums[g * heads : (g + 1) * heads] for g in range(2)]
     variance = jnp.concatenate(sums, axis=1) * (1.0 / chans)
     parts = dot(w3, x, NT)
     scores = parts[:heads] + (parts[heads : 2 * heads] + parts[2 * heads : 3 * heads])
@@ -107,6 +100,8 @@
     ex_far,
     pk_rs,
     pk_ss,
+    pk_ms,
+    pk_mr,
     ms_rs,
     ms_sx,
     ms_up,
@@ -278,20 +273,19 @@
             pl.when(down_z)(lambda: ex_down(above, q).start())
             ex_mate(above, q).start()
 
-    def peak_copy(o, j):
+    def peak_copy(block, send, receive, j):
         return pltpu.make_async_remote_copy(
-            peaks.at[o], peaks.at[o], pk_ss, pk_rs,
-            device_id=(me_i, j), device_id_type=MESH,
+            block, block, send, receive, device_id=(me_i, j), device_id_type=MESH
         )
 
-    def all_peaks():
-        part = peaks.at[pl.ds(0, pj_count - 1)]
-        return pltpu.make_async_remote_copy(
-            part, part, pk_ss, pk_rs, device_id=(me_i, mate), device_id_type=MESH
-        )
-
-    def others(f):
-        lax.fori_loop(1, pj_count, lambda r, c: (f((me_j + r) % pj_count), c)[1], 0)
+    def own_peaks(r):
+        return peak_copy(peaks.at[core, z], pk_ss, pk_rs, (me_j + CORES * r) % pj_count)
+
+    def line_peaks():
+        return peak_copy(peaks.at[core, pl.ds(0, line - 1)], pk_ss, pk_rs, mate)
+
+    def mate_peaks():
+        return peak_copy(peaks.at[core], pk_ms, pk_mr, mate)
 
     def tell_round(r):
         def tell(i, j):
@@ -311,11 +305,11 @@
     away = jnp.where(across // pair_chans == along // pair_chans, -1.0 / pair_chans, 0.0)
     centring[...] = jnp.where(across == along, 1.0 + away, away).astype(jnp.bfloat16)
     lane = lax.broadcasted_iota(jnp.int32, (heads, rows), 1)
-    peaks[me_j] = jnp.zeros((heads, rows), jnp.float32)
+    peaks[core, z] = jnp.zeros((heads, rows), jnp.float32)
 
     def pair_piece(q):
         pair_in(q).wait()
-        top = peaks[me_j]
+        top = peaks[core, z]
         for t in range(PIECE // TILE):
             scores = tile_scores(pair[q % AHEAD, t * TILE : (t + 1) * TILE], w3, centring[...])
             for k in range(TILE):
@@ -323,7 +317,7 @@
                 peak = jnp.max(one, axis=1, keepdims=True)
                 hold[:, t * TILE + k, :] = jnp.exp(one - peak)
                 top = jnp.where(lane == q * PIECE + t * TILE + k, peak, top)
-        peaks[me_j] = top
+        peaks[core, z] = top
         at = pl.ds(pl.multiple_of(q % share * PIECE, PIECE), PIECE)
         ex[me_j, q // share, :, at, :] = hold[...].astype(jnp.bfloat16)
         pl.when(q + AHEAD < chunks * share)(lambda: pair_in(q + AHEAD).start())
@@ -348,7 +342,7 @@
 
     lax.fori_loop(0, chunks * share, pair_step, 0)
     lax.fori_loop(soon, line - 1, lambda r, c: (next_round(r), c)[1], 0)
-    others(lambda j: peak_copy(me_j, j).start())
+    lax.fori_loop(1, line, lambda r, c: (own_peaks(r).start(), c)[1], 0)
 
     def relays(d, first, last):
         lax.fori_loop(first, last, lambda q, c: (relay(d, q), c)[1], 0)
@@ -413,14 +407,17 @@
         values(p, h, slot_of(p))
         return carry
 
-    lax.fori_loop(0, 4, early_values, 0)
-
-    all_peaks().wait_recv()
-    top = jnp.max(peaks[...], axis=0)
+    lax.fori_loop(0, 2, early_values, 0)
+    line_peaks().wait_recv()
+    mate_peaks().start()
+    lax.fori_loop(2, 4, early_values, 0)
+
+    mate_peaks().wait_recv()
+    top = jnp.max(peaks[...].reshape(pj_count, heads, rows), axis=0)
 
     def turn(o, carry):
         pad = jnp.zeros((128 - heads, rows), jnp.float32)
-        turned[o] = jnp.concatenate([jnp.exp(peaks[o] - top), pad], axis=0).T
+        turned[o] = jnp.concatenate([jnp.exp(peaks[o % CORES, o // CORES] - top), pad], axis=0).T
         return carry
 
     lax.fori_loop(0, pj_count, turn, 0)
@@ -547,7 +544,8 @@
 
     lax.fori_loop(0, seqs // GROUP, close_group, 0)
 
-    all_peaks().wait_send()
+    line_peaks().wait_send()
+    mate_peaks().wait_send()
     msa_copy(0, 0, ms_sx, x_near, yline + 1).wait_send()
     for e in range(yline):
         pl.when(up_y & (y - e >= 0))(
@@ -599,7 +597,7 @@
             pltpu.VMEM((pi_count * 2, seqs // 2, chans, tokens), jnp.bfloat16),
             pltpu.VMEM((pj_count, chunks, heads, CHUNK, cols), jnp.bfloat16),
             pltpu.VMEM((heads, PIECE, cols), jnp.float32),
-            pltpu.VMEM((pj_count, heads, rows), jnp.float32),
+            pltpu.VMEM((CORES, pj_count // CORES, heads, rows), jnp.float32),
             pltpu.VMEM((pj_count, rows, 128), jnp.float32),
             pltpu.VMEM((SLOTS, heads, span + 16, rows), jnp.bfloat16),
             pltpu.VMEM((3, heads, rows, CORES * cols), jnp.bfloat16),
@@ -614,6 +612,8 @@
             dma,
             dma((pj_count // CORES,)),
             dma((pj_count // CORES, 2)),
+            dma,
+            dma,
             dma,
             dma,
             dma((pi_count, 2)),

time: 47.4 us -> 46.6 us (0.983)
  Pallas kernels: 46.3 us -> 45.4 us
    pallas_call x1, Pallas kernels: 46.3 us -> 45.4 us  [body(): pl.pallas_call(functools.partial(kernel, pi_count, pj_count), in_specs=[h...]
where the time goes in v5:
time: 46.6 us; the launch traced here: 46.4 us
  Pallas kernels  45.4 us (97%)
  local copies, waits for them, and re-layouts  0.97 us (2%)
    pallas_call x1, Pallas kernels, body(): pl.pallas_call(functools.partial(kernel, pi_count, pj_count), in_specs=[h...  45.4 us
    unnamed x1, local copies, waits for them, and re-layouts  0.97 us

profile of v5, /device:TPU:1, one launch (start us, length us, event | category | flops | bytes accessed | tf_op | source)
XLA Modules:
  0.0 46.4 jit_solution(12646672060095492937)
XLA Ops:
  0.0 45.4 %layer.1 = bf16[32,64,256]{2,1,0:T(8,128)(2,1)S(1)} custom-call(bf16[256,128,128]{2,1,0:T(8,128)(2,1)} %pair_hbm.1, f32[8,128]{1,0:T(8,128)} %bitcast.5, bf16[32,64,256]{2,1,0:T(8,128)(2,1)} %msa_hbm.1, f32[1,64]{1,0:T(1,128)} %bitcast.6, f32[1,64]{1,0:T(1,128)} %bitcast.7, bf16[64,256]{1,0:T(8,128)(2,1)} %payload_hbm.1, bf16[64,256]{1,0:T(8,128)(2,1)} %switch_hbm.1, ...), custom_call_target="tpu_custom_call" | custom-call | tf_op jit(solution)/shard_map/layer/pallas_call | solution.py:580
  45.4 1.0 %copy.10 = bf16[32,64,256]{2,1,0:T(8,128)(2,1)} copy(bf16[32,64,256]{2,1,0:T(8,128)(2,1)S(1)} %layer.1) | data formatting | bytes 2097152

commit v6 on v5

--- a/solution.py
+++ b/solution.py
@@ -17,7 +17,6 @@
 GROUP = 16
 AHEAD = 3
 SLOTS = 4
-SOON = 5
 HELD = 3
 VMEM_LIMIT = 61 << 20
 
@@ -332,8 +331,6 @@
         pair_piece(q)
         pl.when(q % share == share - 1)(lambda: send_own(q // share))
 
-        pl.when((q >= SOON) & (q % 2 == 1))(lambda: relay(1, (q - SOON) // 2))
-
         @pl.when((q % 2 == 1) & (q >= 3) & (q < 3 + 2 * soon))
         def _():
             next_round((q - 3) // 2)
@@ -369,7 +366,7 @@
         column = jnp.sum(jnp.where(diagonal, ref[...], 0.0), axis=1, keepdims=True)
         spread[k] = jnp.broadcast_to(column, (chans, rows))
 
-    relays(1, (chunks - SOON + 1) // 2, chunks - 2)
+    relays(1, 0, chunks - 2)
     lax.fori_loop(0, seqs // GROUP, gate_group, 0)
     relays(1, chunks - 2, chunks)
     first_relays()

time: 46.6 us -> 46.6 us (level)
  no operation moved by 1% of the time
where the time goes in v6:
time: 46.6 us; the launch traced here: 46.4 us
  Pallas kernels  45.4 us (97%)
  local copies, waits for them, and re-layouts  0.97 us (2%)
    pallas_call x1, Pallas kernels, body(): pl.pallas_call(functools.partial(kernel, pi_count, pj_count), in_specs=[h...  45.4 us
    unnamed x1, local copies, waits for them, and re-layouts  0.97 us

profile of v6, /device:TPU:1, one launch (start us, length us, event | category | flops | bytes accessed | tf_op | source)
XLA Modules:
  0.0 46.4 jit_solution(14970233108706317596)
XLA Ops:
  0.0 45.4 %layer.1 = bf16[32,64,256]{2,1,0:T(8,128)(2,1)S(1)} custom-call(bf16[256,128,128]{2,1,0:T(8,128)(2,1)} %pair_hbm.1, f32[8,128]{1,0:T(8,128)} %bitcast.5, bf16[32,64,256]{2,1,0:T(8,128)(2,1)} %msa_hbm.1, f32[1,64]{1,0:T(1,128)} %bitcast.6, f32[1,64]{1,0:T(1,128)} %bitcast.7, bf16[64,256]{1,0:T(8,128)(2,1)} %payload_hbm.1, bf16[64,256]{1,0:T(8,128)(2,1)} %switch_hbm.1, ...), custom_call_target="tpu_custom_call" | custom-call | tf_op jit(solution)/shard_map/layer/pallas_call | solution.py:577
  45.4 1.0 %copy.10 = bf16[32,64,256]{2,1,0:T(8,128)(2,1)} copy(bf16[32,64,256]{2,1,0:T(8,128)(2,1)S(1)} %layer.1) | data formatting | bytes 2097152
